TPU v7x, 32 devices: a 4x4x1 block of a 4x4x8 slice. The times are simulated.
32 devices in a mesh: dp: 1 (over z), cp: 32 (over y, x, core).
Axes of the slice: x: 4, y: 4, z: 1, core: 2. Of those that a mesh axis runs over, the one named last changes fastest.
The devices are a block of a 4x4x8 slice.
Arguments:
- q_tokens: bfloat16 [2048, 12, 128], P(('dp', 'cp'))
- k_tokens: bfloat16 [2048, 2, 128], P(('dp', 'cp'))
- v_tokens: bfloat16 [2048, 2, 128], P(('dp', 'cp'))
- d_out: bfloat16 [2048, 12, 128], P(('dp', 'cp'))
- key_valid: int32 [2048], P(('dp', 'cp'))
- cu_seqlens: int32 [3], P('dp')
Outputs:
- output 1: bfloat16 [2048, 12, 128], P(('dp', 'cp'))
- output 2: float32 [2048, 12], P(('dp', 'cp'))
- output 3: bfloat16 [2048, 12, 128], P(('dp', 'cp'))
- output 4: bfloat16 [2048, 2, 128], P(('dp', 'cp'))
- output 5: bfloat16 [2048, 2, 128], P(('dp', 'cp'))
All inputs are finite; a program needn't handle non-finite values.
Results may differ from a plain program's by a relative error of at most 0.00866085.
Values are sent between devices in bfloat16 or wider.
A program may use at most 768 MiB of HBM per device.

v0:
```python
import jax
import jax.numpy as jnp
from jax import lax
from jax.sharding import PartitionSpec as P

MASK_FILL = -1.0e30


def token_coords(cu_seqlens, rank_ids, local_ids, cp_size):
    starts = cu_seqlens[:-1] // cp_size
    doc_id = jnp.sum((local_ids[..., None] >= starts).astype(jnp.int32), axis=-1) - 1
    seg_start = cu_seqlens[doc_id]
    piece_len = (cu_seqlens[doc_id + 1] - seg_start) // (2 * cp_size)
    within = local_ids - seg_start // cp_size
    in_upper = (within >= piece_len).astype(jnp.int32)
    piece_idx = rank_ids + in_upper * (2 * cp_size - 1 - 2 * rank_ids)
    position = seg_start + piece_idx * piece_len + within - in_upper * piece_len
    return doc_id, position


def solution(mesh):
    cp_size = mesh.shape['cp']
    tok_spec = P(('dp', 'cp'), None, None)
    lse_spec = P(('dp', 'cp'), None)
    row_spec = P(('dp', 'cp'))
    bound_spec = P('dp')

    def local_attention(q_loc, k_loc, v_loc, do_loc, valid_loc, cu_loc):
        tok_count, n_heads, head_dim = q_loc.shape
        kv_heads = k_loc.shape[1]
        group_size = n_heads // kv_heads
        score_scale = head_dim ** -0.5
        my_rank = lax.axis_index('cp')
        local_ids = jnp.arange(tok_count)
        doc_q, pos_q = token_coords(cu_loc, my_rank, local_ids, cp_size)
        rank_grid = jnp.broadcast_to(jnp.arange(cp_size)[:, None], (cp_size, tok_count))
        local_grid = jnp.broadcast_to(local_ids[None, :], (cp_size, tok_count))
        doc_all, pos_all = token_coords(cu_loc, rank_grid, local_grid, cp_size)
        k_all = lax.all_gather(k_loc, 'cp')
        v_all = lax.all_gather(v_loc, 'cp')
        ok_all = lax.all_gather(valid_loc, 'cp') > 0
        q_grouped = q_loc.reshape(tok_count, kv_heads, group_size, head_dim)
        do_grouped = do_loc.reshape(tok_count, kv_heads, group_size, head_dim)
        key_xs = (k_all, v_all, doc_all, pos_all, ok_all)

        def block_scores(k_blk, doc_k, pos_k, ok_k):
            allowed = (doc_q[:, None] == doc_k[None, :]) & (pos_k[None, :] <= pos_q[:, None]) & ok_k[None, :]
            scores = jnp.einsum('qhgd,khd->hgqk', q_grouped, k_blk, preferred_element_type=jnp.float32) * score_scale
            return jnp.where(allowed, scores, MASK_FILL), allowed

        def fwd_step(run_state, blk_data):
            m_run, l_run, acc_run = run_state
            k_blk, v_blk, doc_k, pos_k, ok_k = blk_data
            scores, allowed = block_scores(k_blk, doc_k, pos_k, ok_k)
            m_new = jnp.maximum(m_run, jnp.max(scores, axis=-1))
            weights = jnp.where(allowed, jnp.exp(scores - m_new[..., None]), 0.0)
            rescale = jnp.exp(m_run - m_new)
            l_new = rescale * l_run + jnp.sum(weights, axis=-1)
            acc_new = acc_run * rescale[..., None] + jnp.einsum('hgqk,khd->hgqd', weights.astype(jnp.bfloat16), v_blk, preferred_element_type=jnp.float32)
            return (m_new, l_new, acc_new), None

        m_init = jnp.full((kv_heads, group_size, tok_count), MASK_FILL, jnp.float32)
        l_init = jnp.zeros((kv_heads, group_size, tok_count), jnp.float32)
        acc_init = jnp.zeros((kv_heads, group_size, tok_count, head_dim), jnp.float32)
        m_fin, l_fin, acc_fin = lax.scan(fwd_step, (m_init, l_init, acc_init), key_xs)[0]
        has_key = l_fin > 0
        safe_den = jnp.where(has_key, l_fin, 1.0)
        out_hgqd = jnp.where(has_key[..., None], acc_fin / safe_den[..., None], 0.0)
        out_grouped = jnp.transpose(out_hgqd, (2, 0, 1, 3)).astype(jnp.bfloat16)
        lse_hgq = jnp.where(has_key, m_fin + jnp.log(safe_den), 0.0)
        row_delta = jnp.einsum('qhgd,qhgd->hgq', do_grouped, out_grouped, preferred_element_type=jnp.float32)

        def bwd_step(dq_run, blk_data):
            k_blk, v_blk, doc_k, pos_k, ok_k = blk_data
            scores, allowed = block_scores(k_blk, doc_k, pos_k, ok_k)
            weights = jnp.where(allowed, jnp.exp(scores - lse_hgq[..., None]), 0.0)
            d_prob = jnp.einsum('qhgd,khd->hgqk', do_grouped, v_blk, preferred_element_type=jnp.float32)
            d_score = (weights * (d_prob - row_delta[..., None])).astype(jnp.bfloat16)
            dq_new = dq_run + jnp.einsum('hgqk,khd->qhgd', d_score, k_blk, preferred_element_type=jnp.float32)
            dk_blk = jnp.einsum('hgqk,qhgd->khd', d_score, q_grouped, preferred_element_type=jnp.float32)
            dv_blk = jnp.einsum('hgqk,qhgd->khd', weights.astype(jnp.bfloat16), do_grouped, preferred_element_type=jnp.float32)
            return dq_new, (dk_blk, dv_blk)

        dq_init = jnp.zeros((tok_count, kv_heads, group_size, head_dim), jnp.float32)
        dq_fin, kv_parts = lax.scan(bwd_step, dq_init, key_xs)
        dk_own = lax.psum_scatter(kv_parts[0], 'cp', scatter_dimension=0, tiled=False)
        dv_own = lax.psum_scatter(kv_parts[1], 'cp', scatter_dimension=0, tiled=False)
        attn_out = out_grouped.reshape(tok_count, n_heads, head_dim)
        log_sumexp = jnp.transpose(lse_hgq, (2, 0, 1)).reshape(tok_count, n_heads)
        d_query = (dq_fin * score_scale).astype(jnp.bfloat16).reshape(tok_count, n_heads, head_dim)
        d_key = (dk_own * score_scale).astype(jnp.bfloat16)
        d_value = dv_own.astype(jnp.bfloat16)
        return attn_out, log_sumexp, d_query, d_key, d_value

    return jax.shard_map(local_attention, mesh=mesh, in_specs=(tok_spec, tok_spec, tok_spec, tok_spec, row_spec, bound_spec), out_specs=(tok_spec, lse_spec, tok_spec, tok_spec, tok_spec), check_vma=False)
```

profile of v0, /device:TPU:97, one launch (start us, length us, event | category | flops | bytes accessed | tf_op | source)
XLA Modules:
  0.0 417.1 jit_solution(10833114140398941573)
XLA Ops:
  7.2 1.4 copy.37
  8.8 1.4 copy.38
  11.2 49.8 %all-reduce = s32[2048]{0:T(1024)S(1)} all-reduce(s32[2048]{0:T(1024)S(1)} %dynamic-update-slice), channel_id=2, replica_groups=mesh['dp'=1,'cp'=32] {'cp'}, use_global_device_ids=true, to_apply=%add | all-reduce | flops 2048 | bytes 16384
  61.2 1.4 fusion.62
  63.4 1.9 fusion.56
  65.3 2.0 fusion.47
  67.3 1.3 copy.39
  68.7 23.3 %all-gather.8.cloned.1.call-done = bf16[2048,2,128]{2,0,1:T(8,128)(2,1)} async-done(((bf16[64,2,128]{2,0,1:T(8,128)(2,1)}), bf16[2048,2,128]{2,0,1:T(8,128)(2,1)}) %all-gather.8.cloned.1.call-update) | async-done | bytes 1048592 | tf_op jit(solution)/shard_map/all_gather | solution.py:40
  92.0 2.3 copy.40
  94.3 56.5 %while.30 = (s32[]{:T(128)}, f32[2,6,64]{2,1,0:T(8,128)S(1)}, f32[2,6,64]{2,1,0:T(8,128)S(1)}, f32[2,6,64,128]{3,2,1,0:T(8,128)S(1)}, s32[64]{0:T(128)S(1)}, /*i...) while((s32[]{:T(128)}, f32[2,6,64]{2,1,0:T(8,128)S(1)}, ...), condition=%wide.region_5.6_spmd.clone, body=%wide.region_2.5_spmd.clone.sunk | while | flops 25923332 | bytes 1710941 | solution.py:65
  94.9 1.1 convolution_add_fusion.2
  98.4 1.1 convolution_add_fusion.2
  100.2 1.1 convolution_add_fusion.2
  102.0 1.1 convolution_add_fusion.2
  103.7 1.1 convolution_add_fusion.2
  105.5 1.1 convolution_add_fusion.2
  112.6 1.1 convolution_add_fusion.2
  121.4 1.1 convolution_add_fusion.2
  130.2 1.1 convolution_add_fusion.2
  139.0 1.1 convolution_add_fusion.2
  147.9 1.1 convolution_add_fusion.2
  151.8 114.5 %while.31 = (s32[]{:T(128)}, f32[64,2,6,128]{3,0,2,1:T(8,128)S(1)}, f32[32,64,2,128]{3,1,2,0:T(8,128)}, f32[32,64,2,128]{3,1,2,0:T(8,128)}, bf16[32,64,2,128]{3,...) while((s32[]{:T(128)}, f32[64,2,6,128]{3,0,2,1:T(8,128)S(1)}, ...), condition=%wide.region_7.8_spmd.clone, body=%wide.region_6.7_spmd.clone.sunk | while | flops 63520768 | bytes 2812791 | solution.py:85
  268.3 66.8 %reduce-scatter.3.cloned.1.call-done = f32[1,64,2,128]{3,1,2,0:T(8,128)} async-done(((f32[32,64,2,128]{3,1,2,0:T(8,128)}), f32[1,64,2,128]{3,1,2,0:T(8,128)}) %reduce-scatter.3.cloned.1.call-update) | async-done | bytes 65552 | tf_op jit(solution)/shard_map/reduce_scatter | solution.py:86
  336.6 72.5 %reduce-scatter.5.cloned.1.call-done = f32[1,64,2,128]{3,1,2,0:T(8,128)} async-done(((f32[32,64,2,128]{3,1,2,0:T(8,128)}), f32[1,64,2,128]{3,1,2,0:T(8,128)}) %reduce-scatter.5.cloned.1.call-update) | async-done | bytes 65552 | tf_op jit(solution)/shard_map/reduce_scatter | solution.py:87
  (569 shorter events, 162.4 us)
Async XLA Ops:
  7.2 60.1 %all-gather.6.cloned.1.call-start = ((), (), s32[]{:S(2)}) async-start(), calls=%async_computation.4 | async-start | bytes 1081344 | tf_op jit(solution)/shard_map/all_gather | solution.py:39
  8.7 83.3 %all-gather.8.cloned.1.call-start = ((), (), s32[]{:S(2)}) async-start(), calls=%async_computation.5 | async-start | bytes 1081344 | tf_op jit(solution)/shard_map/all_gather | solution.py:40
  10.2 324.9 %reduce-scatter.3.cloned.1.call-start = ((), (), s32[]{:S(2)}) async-start(), calls=%async_computation.2 | async-start | bytes 2162688 | tf_op jit(solution)/shard_map/reduce_scatter | solution.py:86
  67.3 27.0 %copy-start.1 = (bf16[64,12,128]{2,0,1:T(8,128)(2,1)S(1)}, bf16[64,12,128]{2,0,1:T(8,128)(2,1)}, u32[]{:S(2)}) copy-start(bf16[64,12,128]{2,0,1:T(8,128)(2,1)} %param.10) | copy-start | bytes 589828
  94.3 56.5 %copy-start = (bf16[64,12,128]{2,0,1:T(8,128)(2,1)S(1)}, bf16[64,12,128]{2,0,1:T(8,128)(2,1)}, u32[]{:S(2)}) copy-start(bf16[64,12,128]{2,0,1:T(8,128)(2,1)} %param.13) | copy-start | bytes 589828
  266.3 142.8 %reduce-scatter.5.cloned.1.call-start = ((), (), s32[]{:S(2)}) async-start(), calls=%async_computation.3 | async-start | bytes 2162688 | tf_op jit(solution)/shard_map/reduce_scatter | solution.py:87
Sparse Core Ops, SparseCore 0:
  10.7 41.7 all-gather.5
  55.2 36.7 all-gather.7
  266.4 68.6 reduce-scatter.2
  338.3 70.7 reduce-scatter.4
where the time goes:
time: 422 us; the launch traced here: 417 us
  waiting for transfers between devices  163 us (39%)
  matrix products  155 us (37%)
  blocking collectives  49.8 us (12%)
  other arithmetic  17.7 us (4%)
  between operations  13.9 us (3%)
  local copies, waits for them, and re-layouts  12.3 us (3%)
  loops' own time  4.25 us (1%)
    reduce_scatter x1, waiting for transfers between devices, local_attention(): lax.psum_scatter(kv_parts[1], 'cp', scatter_dimension=0, tiled=False)  72.5 us
    reduce_scatter x1, waiting for transfers between devices, local_attention(): lax.psum_scatter(kv_parts[0], 'cp', scatter_dimension=0, tiled=False)  66.8 us
    unnamed x1, blocking collectives  49.8 us
    dot_general x32, matrix products, fwd_step(): jnp.einsum('hgqk,khd->hgqd', weights.astype(jnp.bfloat16), v_blk, preferr...  35.8 us
    dot_general x32, matrix products, bwd_step(): jnp.einsum('qhgd,khd->hgqk', do_grouped, v_blk, preferred_element_type=jn...  34.5 us
    dot_general x32, matrix products, bwd_step(): jnp.einsum('hgqk,qhgd->khd', d_score, q_grouped, preferred_element_type=j...  27.4 us
    dot_general x32, matrix products, bwd_step(): jnp.einsum('hgqk,qhgd->khd', weights.astype(jnp.bfloat16), do_grouped, pr...  27.2 us
    all_gather x1, waiting for transfers between devices, local_attention(): v_all = lax.all_gather(v_loc, 'cp')  23.3 us
  transfers between devices with their start and end apart: 4, of which 3 were waited for; matrix products, arithmetic and copies ran while one was open for 3% of the time, Pallas kernels for 0%

commit v1 on v0

v1 whole, which is shorter than its diff:
```python
import functools
import math

import jax
import jax.numpy as jnp
from jax import lax
from jax.experimental import pallas as pl
from jax.experimental.pallas import tpu as pltpu
from jax.sharding import PartitionSpec as P

MESH = pl.DeviceIdType.MESH
NEG = -(2.0 ** 126)
CORES = 2
SIDE = 4
LEVELS = (
    ((0, 0),),
    ((1, 0), (3, 0), (0, 1), (0, 3)),
    ((2, 0), (0, 2), (1, 1), (1, 3), (3, 1), (3, 3)),
    ((2, 1), (2, 3), (1, 2), (3, 2)),
    ((2, 2),),
)
BLOCKS = tuple(blk for level in LEVELS for blk in level)
SLOT = {blk: i for i, blk in enumerate(BLOCKS)}
NBLK = len(BLOCKS)
NT = (((1,), (1,)), ((), ()))
TN = (((0,), (0,)), ((), ()))


def dot(a, b, dims=(((1,), (0,)), ((), ()))):
    return lax.dot_general(a, b, dims, preferred_element_type=jnp.float32)


def frame(X, blk):
    return blk if X == 0 else (blk[1], blk[0])


def unframe(X, a, b):
    return (a, b) if X == 0 else (b, a)


def routes(X, blk, o):
    a, b = frame(X, blk)
    out = []
    if b == 0:
        if a == 3 and o == 0:
            out.append((1, 0))
        if a == 1 and o == 1:
            out.append((-1, 0))
        if a == 0:
            out += [(1, 0), (-1, 0)]
        out += [(0, 1), (0, -1)]
    elif b == 3 and o == 0:
        out.append((0, 1))
    elif b == 1 and o == 1:
        out.append((0, -1))
    return [unframe(X, *step) for step in out]


RKEYS = []
for _a in range(SIDE):
    RKEYS += [('rb', _a, 0), ('rb', _a, 1)]
    RKEYS += [('fb', _a, _o, _s) for _o in range(2) for _s in (1, -1)]
RKEYS += [('ra', 0), ('ra', 1)]
RKEYS += [('fa', _o, _s) for _o in range(2) for _s in (1, -1)]
RIDX = {key: i for i, key in enumerate(RKEYS)}


def kernel(cp, n_docs, scale, q_hbm, k_hbm, v_hbm, do_hbm, val_hbm, cu_hbm,
           o_hbm, lse_hbm, dq_hbm, dk_hbm, dv_hbm,
           kin, kf32, oth, kv, kaug, qaug, dob, dot_t, sbuf, dpbuf, pbuf, dsbuf, part, rbuf,
           ost, dqst, lsest, kvsend, kvrecv, tmp32, outb, m_ref, l_ref, o_t, valv, cus,
           loc_sem, pair_send, pair_recv, ag_send, ag_recv, rs_send, rs_recv):
    tok = valv.shape[1]
    grp = ost.shape[0] // CORES
    rows = CORES * grp * tok
    hd = kin.shape[-1]
    keys = CORES * tok
    me = lax.axis_index('cp')
    core = lax.rem(me, CORES)
    chip = lax.div(me, CORES)
    cx = lax.rem(chip, SIDE)
    cy = lax.div(chip, SIDE)
    partner = me + 1 - 2 * core

    def chip_at(dx, dy):
        return lax.rem(cy + dy + SIDE, SIDE) * SIDE + lax.rem(cx + dx + SIDE, SIDE)

    def nbr(step):
        return {'cp': chip_at(*step) * CORES + core}

    mine = core * grp
    theirs = (1 - core) * grp
    to_partner = {'cp': partner}

    c_k = pltpu.make_async_copy(k_hbm, kin.at[0], loc_sem.at[0])
    c_v = pltpu.make_async_copy(v_hbm, kin.at[1], loc_sem.at[1])
    c_val = pltpu.make_async_copy(val_hbm, valv, loc_sem.at[2])
    c_cu = pltpu.make_async_copy(cu_hbm, cus, loc_sem.at[3])
    c_q = pltpu.make_async_copy(q_hbm.at[pl.ds(mine, grp)], qaug.at[0:grp, :, 0:hd], loc_sem.at[4])
    c_do = pltpu.make_async_copy(do_hbm.at[pl.ds(mine, grp)], dob.at[0:grp], loc_sem.at[5])
    for c in (c_k, c_v, c_val, c_cu, c_q, c_do):
        c.start()

    barrier = pltpu.get_barrier_semaphore()
    peers = [to_partner] + [nbr(s) for s in ((1, 0), (-1, 0), (0, 1), (0, -1))]
    for peer in peers:
        pl.semaphore_signal(barrier, inc=1, device_id=peer, device_id_type=MESH)

    sends = []

    def remote(src, dst, ssem, rsem, dev):
        copy = pltpu.make_async_remote_copy(src_ref=src, dst_ref=dst, send_sem=ssem, recv_sem=rsem,
                                            device_id=dev, device_id_type=MESH)
        return copy

    def push(src, dst, ssem, rsem, dev):
        copy = remote(src, dst, ssem, rsem, dev)
        copy.start()
        sends.append(copy)
        return copy

    for c in (c_k, c_v, c_val):
        c.wait()
    sub = lax.broadcasted_iota(jnp.int32, (tok, tok), 0)
    lane = lax.broadcasted_iota(jnp.int32, (tok, tok), 1)
    vcol = jnp.sum(jnp.where(sub == lane, jnp.broadcast_to(valv[...], (tok, tok)), 0), axis=1, keepdims=True)
    lane0 = lax.broadcasted_iota(jnp.int32, (tok, hd), 1) == 0
    bad = lane0 & (jnp.broadcast_to(vcol, (tok, hd)) <= 0)
    for X in range(2):
        kf32[X] = kin[X].astype(jnp.float32)
    for X in range(2):
        h0 = kf32[X, pl.ds(0, tok, stride=2), :]
        h1 = kf32[X, pl.ds(1, tok, stride=2), :]
        own = jnp.where(core == 0, h0, h1)
        other = jnp.where(core == 0, h1, h0)
        if X == 0:
            own = jnp.where(bad, jnp.inf, own)
            other = jnp.where(bad, jnp.inf, other)
        kv[X, 0, 0] = own.astype(jnp.bfloat16)
        oth[X] = other.astype(jnp.bfloat16)

    pl.semaphore_wait(barrier, len(peers))

    ag_count = [0]

    def forward(X, blk, o):
        for step in routes(X, blk, o):
            dst_blk = ((blk[0] - step[0]) % SIDE, (blk[1] - step[1]) % SIDE)
            s = SLOT[dst_blk]
            push(kv.at[X, SLOT[blk], o], kv.at[X, s, o], ag_send.at[ag_count[0]], ag_recv.at[X, s, o], nbr(step))
            ag_count[0] += 1

    def arrive(X, blk, o):
        s = SLOT[blk]
        remote(kv.at[X, s, o], kv.at[X, s, o], ag_send.at[0], ag_recv.at[X, s, o], to_partner).wait_recv()

    for X in range(2):
        push(oth.at[X], kv.at[X, 0, 1], pair_send.at[X], ag_recv.at[X, 0, 1], to_partner)
    for X in range(2):
        forward(X, (0, 0), 0)
    x_q = push(q_hbm.at[pl.ds(theirs, grp)], qaug.at[grp:2 * grp, :, 0:hd], pair_send.at[2], pair_recv.at[2], to_partner)
    x_do = push(do_hbm.at[pl.ds(theirs, grp)], dob.at[grp:2 * grp], pair_send.at[3], pair_recv.at[3], to_partner)

    t_row = lax.broadcasted_iota(jnp.int32, (tok, hd), 0)
    t_lane = lax.broadcasted_iota(jnp.int32, (tok, hd), 1)
    for o in range(CORES):
        hot = jnp.where(t_lane == t_row + o * tok, 1.0, 0.0).astype(jnp.bfloat16)
        for h in range(grp):
            qaug[o * grp + h, :, hd:2 * hd] = hot

    c_cu.wait()
    bounds = [cus[0, d] for d in range(n_docs + 1)]

    def coords(t):
        seg = jnp.full(t.shape, bounds[0], jnp.int32)
        loc = jnp.full(t.shape, lax.div(bounds[0], cp), jnp.int32)
        plen = jnp.full(t.shape, lax.div(bounds[1] - bounds[0], 2 * cp), jnp.int32)
        for d in range(1, n_docs):
            first = lax.div(bounds[d], cp)
            hit = t >= first
            seg = jnp.where(hit, bounds[d], seg)
            loc = jnp.where(hit, first, loc)
            plen = jnp.where(hit, lax.div(bounds[d + 1] - bounds[d], 2 * cp), plen)
        within = t - loc
        up = within >= plen
        base = seg + within + jnp.where(up, (2 * cp - 2) * plen, 0)
        return seg, base, jnp.where(up, -plen, plen)

    _, key_base, key_slope = coords(t_row)
    lane_q = lax.broadcasted_iota(jnp.int32, (8, keys), 1)
    seg_q, base_q, slope_q = coords(lax.rem(lane_q, tok))
    rank_q = jnp.where(lane_q < tok, me, partner)
    pos_q = base_q + rank_q * slope_q
    lo_b = jnp.broadcast_to(seg_q[0:1], (tok, keys))
    hi_b = jnp.broadcast_to(pos_q[0:1], (tok, keys))

    def prepare(blk):
        s = SLOT[blk]
        for o in range(CORES):
            rank = chip_at(*blk) * CORES + (core if o == 0 else 1 - core)
            pos = key_base + rank * key_slope
            kf = kv[0, s, o].astype(jnp.float32)
            invalid = jnp.broadcast_to(kf[:, 0:1], (tok, keys)) == jnp.inf
            seen = (pos >= lo_b) & (pos <= hi_b) & jnp.logical_not(invalid)
            kaug[s, o * tok:(o + 1) * tok, 0:hd] = jnp.where(kf == jnp.inf, 0.0, kf).astype(jnp.bfloat16)
            kaug[s, o * tok:(o + 1) * tok, hd:2 * hd] = jnp.where(seen, 0.0, NEG).astype(jnp.bfloat16)

    c2 = scale * math.log2(math.e)

    def scores(level):
        lo, n = SLOT[level[0]], len(level)
        for blk in level:
            prepare(blk)
        ka = kaug[lo:lo + n].reshape(n * keys, 2 * hd)
        sbuf[lo:lo + n] = dot(ka, qaug[...].reshape(rows, 2 * hd), NT).reshape(n, keys, rows)

    def grads_p(level):
        lo, n = SLOT[level[0]], len(level)
        vb = kv[1, lo:lo + n].reshape(n * keys, hd)
        dpbuf[lo:lo + n] = dot(vb, dob[...].reshape(rows, hd), NT).reshape(n, keys, rows)

    def softmax(level, first):
        lo, n = SLOT[level[0]], len(level)
        mx = jnp.max(sbuf[lo:lo + n].reshape(n * keys, rows), axis=0, keepdims=True)
        if first:
            m_new = mx
        else:
            m_old = m_ref[...]
            m_new = jnp.maximum(m_old, mx)
            alpha = jnp.exp2((m_old - m_new) * c2)
        m_ref[...] = m_new
        mc = m_new * c2
        total = None
        for i in range(n):
            p = jnp.exp2(sbuf[lo + i] * c2 - mc)
            pbuf[lo + i] = p.astype(jnp.bfloat16)
            part_sum = jnp.sum(p, axis=0, keepdims=True)
            total = part_sum if total is None else total + part_sum
        pv = dot(kv[1, lo:lo + n].reshape(n * keys, hd), pbuf[lo:lo + n].reshape(n * keys, rows), TN)
        if first:
            l_ref[...] = total
            o_t[...] = pv
        else:
            l_ref[...] = l_ref[...] * alpha + total
            o_t[...] = o_t[...] * alpha + pv

    for X in range(2):
        arrive(X, (0, 0), 1)
        forward(X, (0, 0), 1)
    c_q.wait()
    x_q.wait_recv()
    scores(LEVELS[0])
    c_do.wait()
    x_do.wait_recv()
    dot_t[...] = jnp.transpose(dob[...].reshape(rows, hd).astype(jnp.float32))
    softmax(LEVELS[0], True)
    grads_p(LEVELS[0])
    for level in LEVELS[1:]:
        for o in range(CORES):
            for blk in level:
                for X in range(2):
                    arrive(X, blk, o)
                    forward(X, blk, o)
        scores(level)
        softmax(level, False)
        grads_p(level)

    m_fin, l_fin = m_ref[...], l_ref[...]
    has_key = m_fin > NEG * 0.5
    safe = jnp.where(has_key, l_fin, 1.0)
    o_b = jnp.where(has_key, o_t[...] / safe, 0.0).astype(jnp.bfloat16).astype(jnp.float32)
    o_t[...] = o_b
    delta = jnp.sum(o_b * dot_t[...], axis=0, keepdims=True)
    lse = jnp.where(has_key, m_fin * scale + jnp.log(safe), 0.0)
    lse2 = jnp.where(has_key, m_fin * c2 + jnp.log2(safe), 0.0)

    rs_items = []

    def rsend(X, blk, o, key, step):
        i = RIDX[key]
        push(part.at[X, SLOT[blk], o], rbuf.at[X, i], rs_send.at[X, i], rs_recv.at[X, i], nbr(unframe(X, *step)))

    def rwait(X, key):
        i = RIDX[key]
        remote(rbuf.at[X, i], rbuf.at[X, i], rs_send.at[X, i], rs_recv.at[X, i], to_partner).wait_recv()
        return rbuf[X, i]

    def immediate(X, blk):
        a, b = frame(X, blk)
        if b == 2:
            rsend(X, blk, 0, ('rb', a, 0), (0, -1))
            rsend(X, blk, 1, ('rb', a, 1), (0, 1))
        elif b == 3:
            rsend(X, blk, 1, ('fb', a, 1, 1), (0, -1))
        elif b == 1:
            rsend(X, blk, 0, ('fb', a, 0, -1), (0, 1))

    def relay_b(X, a):
        for b, o, step, sgn in ((3, 0, -1, 1), (1, 1, 1, -1)):
            blk = unframe(X, a, b)
            part[X, SLOT[blk], o] += rwait(X, ('rb', a, o))
            rsend(X, blk, o, ('fb', a, o, sgn), (0, step))

    def gather_b(X, a, o):
        blk = unframe(X, a, 0)
        part[X, SLOT[blk], o] += rwait(X, ('fb', a, o, 1)) + rwait(X, ('fb', a, o, -1))
        return blk

    def relay_a(X, a, o):
        blk = gather_b(X, a, o)
        if a == 2:
            rsend(X, blk, o, ('ra', o), (-1 if o == 0 else 1, 0))
        else:
            if (a == 3) == (o == 0):
                part[X, SLOT[blk], o] += rwait(X, ('ra', o))
            rsend(X, blk, o, ('fa', o, 1 if a == 3 else -1), (-1 if a == 3 else 1, 0))

    dob2 = dob[...].reshape(rows, hd)

    def backward(blk):
        s = SLOT[blk]
        p = jnp.exp2(sbuf[s] * c2 - lse2)
        pbuf[s] = p.astype(jnp.bfloat16)
        dsbuf[s] = (p * (dpbuf[s] - delta)).astype(jnp.bfloat16)
        part[1, s] = dot(pbuf[s], dob[...].reshape(rows, hd)).reshape(CORES, tok, hd)
        part[0, s] = dot(dsbuf[s], qaug[:, :, 0:hd].reshape(rows, hd)).reshape(CORES, tok, hd)
        for X in range(2):
            immediate(X, blk)

    for level in (LEVELS[4], LEVELS[3], LEVELS[2]):
        for blk in level:
            backward(blk)
    for X in range(2):
        relay_b(X, 2)
    for blk in LEVELS[1]:
        backward(blk)
    for a in (1, 3, 0):
        for X in range(2):
            relay_b(X, a)
    backward((0, 0))
    for o in range(CORES):
        for X in range(2):
            relay_a(X, 2, o)

    o_rows = jnp.transpose(o_t[...]).astype(jnp.bfloat16).reshape(2 * grp, tok, hd)
    ost[...] = o_rows
    for o in range(CORES):
        for h in range(grp):
            j = (o * grp + h) * tok
            lsest[o, h:h + 1, :] = lse[:, j:j + tok]
    w_o = pltpu.make_async_copy(ost.at[0:grp], o_hbm.at[pl.ds(mine, grp)], loc_sem.at[0])
    w_l = pltpu.make_async_copy(lsest.at[0], lse_hbm.at[core], loc_sem.at[1])
    w_o.start()
    w_l.start()
    x_o = push(ost.at[grp:2 * grp], o_hbm.at[pl.ds(mine, grp)], pair_send.at[4], pair_recv.at[4], to_partner)
    x_l = push(lsest.at[1], lse_hbm.at[core], pair_send.at[5], pair_recv.at[5], to_partner)
    dq_t = dot(kaug[:, :, 0:hd].reshape(NBLK * keys, hd), dsbuf[...].reshape(NBLK * keys, rows), TN)
    dqst[...] = (jnp.transpose(dq_t) * scale).astype(jnp.bfloat16).reshape(2 * grp, tok, hd)
    w_q = pltpu.make_async_copy(dqst.at[0:grp], dq_hbm.at[pl.ds(mine, grp)], loc_sem.at[2])
    w_q.start()
    x_dq = push(dqst.at[grp:2 * grp], dq_hbm.at[pl.ds(mine, grp)], pair_send.at[6], pair_recv.at[6], to_partner)

    for a in (1, 3):
        for o in range(CORES):
            for X in range(2):
                relay_a(X, a, o)

    def final(X, o):
        gather_b(X, 0, o)
        total = part[X, 0, o] + rwait(X, ('fa', o, 1)) + rwait(X, ('fa', o, -1))
        if X == 0:
            total = total * scale
        return total.astype(jnp.bfloat16)

    x_kv = []
    for X in range(2):
        kvsend[X] = final(X, 1)
        x_kv.append(push(kvsend.at[X], kvrecv.at[X], pair_send.at[7 + X], pair_recv.at[7 + X], to_partner))
    owns = [final(X, 0).astype(jnp.float32) for X in range(2)]
    w_kv = []
    for X, out in ((0, dk_hbm), (1, dv_hbm)):
        x_kv[X].wait_recv()
        got = kvrecv[X].astype(jnp.float32)
        tmp32[X, pl.ds(0, tok, stride=2), :] = jnp.where(core == 0, owns[X], got)
        tmp32[X, pl.ds(1, tok, stride=2), :] = jnp.where(core == 0, got, owns[X])
        outb[X] = tmp32[X].astype(jnp.bfloat16)
        w = pltpu.make_async_copy(outb.at[X], out, loc_sem.at[3 + X])
        w.start()
        w_kv.append(w)
    for c in sends:
        c.wait_send()
    for x in (x_o, x_l, x_dq):
        x.wait_recv()
    for w in [w_o, w_l, w_q] + w_kv:
        w.wait()


def solution(mesh):
    cp = mesh.shape['cp']
    tok_spec = P(('dp', 'cp'), None, None)

    def local(q, k, v, do, valid, cu):
        tok, heads, hd = q.shape
        kvh = k.shape[1]
        grp = heads // kvh
        n_docs = cu.shape[0] - 1
        rows = CORES * grp * tok
        keys = CORES * tok
        assert kvh == CORES and cp == CORES * SIDE * SIDE and keys == hd
        bf, f32 = jnp.bfloat16, jnp.float32
        any_spec = pl.BlockSpec(memory_space=pl.ANY)
        n_rs = len(RKEYS)
        flat = lambda x: x.reshape(tok * kvh, hd)
        o, lse, dq, dk, dv = pl.pallas_call(
            functools.partial(kernel, cp, n_docs, hd ** -0.5),
            name='ring_attention',
            out_shape=[
                jax.ShapeDtypeStruct((heads, tok, hd), bf),
                jax.ShapeDtypeStruct((CORES, grp, tok), f32),
                jax.ShapeDtypeStruct((heads, tok, hd), bf),
                jax.ShapeDtypeStruct((tok * kvh, hd), bf),
                jax.ShapeDtypeStruct((tok * kvh, hd), bf),
            ],
            in_specs=[any_spec] * 6,
            out_specs=[any_spec] * 5,
            scratch_shapes=[
                pltpu.VMEM((2, tok * kvh, hd), bf),
                pltpu.VMEM((2, tok * kvh, hd), f32),
                pltpu.VMEM((2, tok, hd), bf),
                pltpu.VMEM((2, NBLK, CORES, tok, hd), bf),
                pltpu.VMEM((NBLK, keys, 2 * hd), bf),
                pltpu.VMEM((CORES * grp, tok, 2 * hd), bf),
                pltpu.VMEM((CORES * grp, tok, hd), bf),
                pltpu.VMEM((hd, rows), f32),
                pltpu.VMEM((NBLK, keys, rows), f32),
                pltpu.VMEM((NBLK, keys, rows), f32),
                pltpu.VMEM((NBLK, keys, rows), bf),
                pltpu.VMEM((NBLK, keys, rows), bf),
                pltpu.VMEM((2, NBLK, CORES, tok, hd), f32),
                pltpu.VMEM((2, n_rs, tok, hd), f32),
                pltpu.VMEM((CORES * grp, tok, hd), bf),
                pltpu.VMEM((CORES * grp, tok, hd), bf),
                pltpu.VMEM((CORES, grp, tok), f32),
                pltpu.VMEM((2, tok, hd), bf),
                pltpu.VMEM((2, tok, hd), bf),
                pltpu.VMEM((2, tok * kvh, hd), f32),
                pltpu.VMEM((2, tok * kvh, hd), bf),
                pltpu.VMEM((1, rows), f32),
                pltpu.VMEM((1, rows), f32),
                pltpu.VMEM((hd, rows), f32),
                pltpu.VMEM((1, tok), jnp.int32),
                pltpu.SMEM((1, n_docs + 1), jnp.int32),
                pltpu.SemaphoreType.DMA((6,)),
                pltpu.SemaphoreType.DMA((9,)),
                pltpu.SemaphoreType.DMA((9,)),
                pltpu.SemaphoreType.DMA((64,)),
                pltpu.SemaphoreType.DMA((2, NBLK, CORES)),
                pltpu.SemaphoreType.DMA((2, n_rs)),
                pltpu.SemaphoreType.DMA((2, n_rs)),
            ],
            compiler_params=pltpu.CompilerParams(
                collective_id=0, has_side_effects=True, vmem_limit_bytes=60 * 1024 * 1024),
        )(q.transpose(1, 0, 2), flat(k), flat(v), do.transpose(1, 0, 2), valid.reshape(1, tok), cu.reshape(1, n_docs + 1))
        back = lambda x: x.reshape(tok, kvh, hd)
        return (o.transpose(1, 0, 2), lse.reshape(heads, tok).transpose(1, 0), dq.transpose(1, 0, 2), back(dk), back(dv))

    return jax.shard_map(
        local, mesh=mesh,
        in_specs=(tok_spec, tok_spec, tok_spec, tok_spec, P(('dp', 'cp')), P('dp')),
        out_specs=(tok_spec, P(('dp', 'cp'), None), tok_spec, tok_spec, tok_spec), check_vma=False)
```

time: 422 us -> 48.1 us (0.11); the launches traced: 417 us -> 47.8 us
  waiting for transfers between devices: 163 us -> 0 us
  matrix products: 155 us -> 0 us
  blocking collectives: 49.8 us -> 0 us
  Pallas kernels: 0 us -> 42.1 us
  other arithmetic: 17.7 us -> 0 us
  between operations: 13.9 us -> 0.65 us
  local copies, waits for them, and re-layouts: 12.3 us -> 5.09 us
  loops' own time: 4.25 us -> 0 us
    dot_general x224 -> x0, matrix products: 155 us -> none  [the longest x32 35.8 us: fwd_step(): jnp.einsum('hgqk,khd->hgqd', weights.astype(jnp.bfloat16), v_blk, preferr...]
    reduce_scatter x2 -> x0, waiting for transfers between devices: 139 us -> none  [the longest x1 72.5 us: local_attention(): lax.psum_scatter(kv_parts[1], 'cp', scatter_dimension=0, tiled=False)]
    unnamed x1 -> x0, blocking collectives: 49.8 us -> none
    pallas_call x0 -> x1, Pallas kernels: none -> 42.1 us  [local(): pl.pallas_call(functools.partial(kernel, cp, n_docs, hd ** (-0.5)), name=...]
    all_gather x2 -> x0, waiting for transfers between devices: 23.3 us -> none  [the longest x1 23.3 us: local_attention(): v_all = lax.all_gather(v_loc, 'cp')]
    and x64 -> x0, other arithmetic: 5.76 us -> none  [block_scores(): (doc_q[:, None] == doc_k[None, :]) & (pos_k[None, :] <= pos_q[:, None])]
    another operation x2 -> x0, loops' own time: 4.25 us -> none  [the longest x1 2.59 us: local_attention(): lax.scan(fwd_step, (m_init, l_init, acc_init), key_xs)[0]]
  transfers between devices with their start and end apart: 4 -> 0, of which waited for: 3 -> 0; matrix products, arithmetic and copies ran while one was open for 3% -> 0% of each run, Pallas kernels for 0% -> 0%
where the time goes in v1:
time: 48.1 us; the launch traced here: 47.8 us
  Pallas kernels  42.1 us (88%)
  local copies, waits for them, and re-layouts  5.09 us (11%)
  between operations  0.65 us (1%)
    pallas_call x1, Pallas kernels, local(): pl.pallas_call(functools.partial(kernel, cp, n_docs, hd ** (-0.5)), name=...  42.1 us
    unnamed x12, local copies, waits for them, and re-layouts  4.49 us

profile of v1, /device:TPU:97, one launch (start us, length us, event | category | flops | bytes accessed | tf_op | source)
XLA Modules:
  0.0 47.8 jit_solution(9895553869977460813)
XLA Ops:
  0.6 42.1 %ring_attention.1 = (bf16[12,64,128]{2,1,0:T(8,128)(2,1)}, f32[2,6,64]{2,1,0:T(8,128)}, bf16[12,64,128]{2,1,0:T(8,128)(2,1)}, bf16[128,128]{1,0:T(8,128)(2,1)}, bf16[128,128]{1,0:T(8,128)(2,1)}) custom-call(bf16[12,64,128]{2,1,0:T(8,128)(2,1)} %bitcast.11, bf16[128,128]{1,0:T(8,128)(2,1)} %bitcast.15, bf16[128,128]{1,0:T(8,128)(2,1)} %bitcast.16, ...), custom_call_target="tpu_custom_call" | custom-call | tf_op jit(solution)/shard_map/ring_attention/pallas_call | solution.py:414
  42.7 0.0 copy-start.3
  42.7 0.7 %copy-done.3 = f32[2,6,64]{2,1,0:T(8,128)S(1)} copy-done((f32[2,6,64]{2,1,0:T(8,128)S(1)}, f32[2,6,64]{2,1,0:T(8,128)}, u32[]{:S(2)}) %copy-start.3) | copy-done | bytes 3096
  43.4 0.6 %reshape.35 = f32[12,64]{1,0:T(8,128)} reshape(f32[2,6,64]{2,1,0:T(8,128)S(1)} %copy-done.3) | data formatting | bytes 6144 | tf_op jit(solution)/shard_map/reshape | solution.py:465
  44.0 0.0 copy-start
  44.0 1.7 %copy.15 = bf16[64,12,128]{2,0,1:T(8,128)(2,1)} copy(bf16[64,12,128]{2,0,1:T(8,128)(2,1)} %bitcast.14) | data formatting | bytes 393216
  45.7 0.0 copy-done
  45.7 0.0 copy-start.2
  45.7 0.7 %copy.16 = bf16[64,12,128]{2,0,1:T(8,128)(2,1)} copy(bf16[64,12,128]{2,0,1:T(8,128)(2,1)S(1)} %bitcast.13) | data formatting | bytes 393216
  46.4 0.1 copy-done.2
  46.5 0.0 copy-start.1
  46.5 0.6 %copy.17 = bf16[64,2,128]{2,1,0:T(2,128)(2,1)} copy(bf16[64,2,128]{2,1,0:T(2,128)(2,1)S(1)} %bitcast.18) | data formatting | bytes 65536
  47.1 0.2 copy-done.1
  47.2 0.6 %copy.18 = bf16[64,2,128]{2,1,0:T(2,128)(2,1)} copy(bf16[64,2,128]{2,1,0:T(2,128)(2,1)S(1)} %bitcast.17) | data formatting | bytes 65536
Async XLA Ops:
  42.7 0.7 %copy-start.3 = (f32[2,6,64]{2,1,0:T(8,128)S(1)}, f32[2,6,64]{2,1,0:T(8,128)}, u32[]{:S(2)}) copy-start(f32[2,6,64]{2,1,0:T(8,128)} %get-tuple-element.11) | copy-start | bytes 9220
  44.0 1.7 %copy-start = (bf16[12,64,128]{2,1,0:T(8,128)(2,1)S(1)}, bf16[12,64,128]{2,1,0:T(8,128)(2,1)}, u32[]{:S(2)}) copy-start(bf16[12,64,128]{2,1,0:T(8,128)(2,1)} %get-tuple-element.12) | copy-start | bytes 589828
  45.7 0.8 %copy-start.2 = (bf16[128,128]{1,0:T(8,128)(2,1)S(1)}, bf16[128,128]{1,0:T(8,128)(2,1)}, u32[]{:S(2)}) copy-start(bf16[128,128]{1,0:T(8,128)(2,1)} %get-tuple-element.13) | copy-start | bytes 98308
  46.5 0.8 %copy-start.1 = (bf16[128,128]{1,0:T(8,128)(2,1)S(1)}, bf16[128,128]{1,0:T(8,128)(2,1)}, u32[]{:S(2)}) copy-start(bf16[128,128]{1,0:T(8,128)(2,1)} %get-tuple-element.14) | copy-start | bytes 98308

commit v2 on v1

--- a/solution.py
+++ b/solution.py
@@ -9,6 +9,7 @@
 from jax.sharding import PartitionSpec as P
 
 MESH = pl.DeviceIdType.MESH
+scope = jax.named_scope
 NEG = -(2.0 ** 126)
 CORES = 2
 SIDE = 4
@@ -66,12 +67,12 @@
 
 
 def kernel(cp, n_docs, scale, q_hbm, k_hbm, v_hbm, do_hbm, val_hbm, cu_hbm,
-           o_hbm, lse_hbm, dq_hbm, dk_hbm, dv_hbm,
+           o_out, lse_out, dq_out, dk_out, dv_out,
            kin, kf32, oth, kv, kaug, qaug, dob, dot_t, sbuf, dpbuf, pbuf, dsbuf, part, rbuf,
-           ost, dqst, lsest, kvsend, kvrecv, tmp32, outb, m_ref, l_ref, o_t, valv, cus,
+           ost, dqst, lsest, kvsend, kvrecv, tmp32, m_ref, l_ref, o_t, valv, cus,
            loc_sem, pair_send, pair_recv, ag_send, ag_recv, rs_send, rs_recv):
     tok = valv.shape[1]
-    grp = ost.shape[0] // CORES
+    grp = ost.shape[0]
     rows = CORES * grp * tok
     hd = kin.shape[-1]
     keys = CORES * tok
@@ -119,8 +120,9 @@
         sends.append(copy)
         return copy
 
-    for c in (c_k, c_v, c_val):
-        c.wait()
+    with scope('load_kv'):
+        for c in (c_k, c_v, c_val):
+            c.wait()
     sub = lax.broadcasted_iota(jnp.int32, (tok, tok), 0)
     lane = lax.broadcasted_iota(jnp.int32, (tok, tok), 1)
     vcol = jnp.sum(jnp.where(sub == lane, jnp.broadcast_to(valv[...], (tok, tok)), 0), axis=1, keepdims=True)
@@ -139,7 +141,8 @@
         kv[X, 0, 0] = own.astype(jnp.bfloat16)
         oth[X] = other.astype(jnp.bfloat16)
 
-    pl.semaphore_wait(barrier, len(peers))
+    with scope('barrier'):
+        pl.semaphore_wait(barrier, len(peers))
 
     ag_count = [0]
 
@@ -168,7 +171,8 @@
         for h in range(grp):
             qaug[o * grp + h, :, hd:2 * hd] = hot
 
-    c_cu.wait()
+    with scope('wait_cu'):
+        c_cu.wait()
     bounds = [cus[0, d] for d in range(n_docs + 1)]
 
     def coords(t):
@@ -244,27 +248,40 @@
             l_ref[...] = l_ref[...] * alpha + total
             o_t[...] = o_t[...] * alpha + pv
 
-    for X in range(2):
-        arrive(X, (0, 0), 1)
-        forward(X, (0, 0), 1)
-    c_q.wait()
-    x_q.wait_recv()
-    scores(LEVELS[0])
-    c_do.wait()
-    x_do.wait_recv()
-    dot_t[...] = jnp.transpose(dob[...].reshape(rows, hd).astype(jnp.float32))
-    softmax(LEVELS[0], True)
-    grads_p(LEVELS[0])
-    for level in LEVELS[1:]:
-        for o in range(CORES):
-            for blk in level:
-                for X in range(2):
-                    arrive(X, blk, o)
-                    forward(X, blk, o)
-        scores(level)
-        softmax(level, False)
-        grads_p(level)
-
+    with scope('pair_kv'):
+        for X in range(2):
+            arrive(X, (0, 0), 1)
+            forward(X, (0, 0), 1)
+    with scope('pair_q'):
+        c_q.wait()
+        x_q.wait_recv()
+    with scope('scores0'):
+        scores(LEVELS[0])
+    with scope('pair_do'):
+        c_do.wait()
+        x_do.wait_recv()
+    with scope('do_t'):
+        dot_t[...] = jnp.transpose(dob[...].reshape(rows, hd).astype(jnp.float32))
+    with scope('softmax0'):
+        softmax(LEVELS[0], True)
+    with scope('grads_p0'):
+        grads_p(LEVELS[0])
+    for i, level in enumerate(LEVELS[1:], 1):
+        with scope('gather%d' % i):
+            for o in range(CORES):
+                for blk in level:
+                    for X in range(2):
+                        arrive(X, blk, o)
+                        forward(X, blk, o)
+        with scope('scores%d' % i):
+            scores(level)
+        with scope('softmax%d' % i):
+            softmax(level, False)
+        with scope('grads_p%d' % i):
+            grads_p(level)
+
+    scope_fin = scope('finish')
+    scope_fin.__enter__()
     m_fin, l_fin = m_ref[...], l_ref[...]
     has_key = m_fin > NEG * 0.5
     safe = jnp.where(has_key, l_fin, 1.0)
@@ -274,7 +291,7 @@
     lse = jnp.where(has_key, m_fin * scale + jnp.log(safe), 0.0)
     lse2 = jnp.where(has_key, m_fin * c2 + jnp.log2(safe), 0.0)
 
-    rs_items = []
+    scope_fin.__exit__(None, None, None)
 
     def rsend(X, blk, o, key, step):
         i = RIDX[key]
@@ -315,8 +332,6 @@
                 part[X, SLOT[blk], o] += rwait(X, ('ra', o))
             rsend(X, blk, o, ('fa', o, 1 if a == 3 else -1), (-1 if a == 3 else 1, 0))
 
-    dob2 = dob[...].reshape(rows, hd)
-
     def backward(blk):
         s = SLOT[blk]
         p = jnp.exp2(sbuf[s] * c2 - lse2)
@@ -329,41 +344,50 @@
 
     for level in (LEVELS[4], LEVELS[3], LEVELS[2]):
         for blk in level:
+            with scope('bwd%d%d' % blk):
+                backward(blk)
+    with scope('relay_b2'):
+        for X in range(2):
+            relay_b(X, 2)
+    for blk in LEVELS[1]:
+        with scope('bwd%d%d' % blk):
             backward(blk)
-    for X in range(2):
-        relay_b(X, 2)
-    for blk in LEVELS[1]:
-        backward(blk)
     for a in (1, 3, 0):
-        for X in range(2):
-            relay_b(X, a)
-    backward((0, 0))
-    for o in range(CORES):
-        for X in range(2):
-            relay_a(X, 2, o)
-
-    o_rows = jnp.transpose(o_t[...]).astype(jnp.bfloat16).reshape(2 * grp, tok, hd)
-    ost[...] = o_rows
-    for o in range(CORES):
-        for h in range(grp):
-            j = (o * grp + h) * tok
-            lsest[o, h:h + 1, :] = lse[:, j:j + tok]
-    w_o = pltpu.make_async_copy(ost.at[0:grp], o_hbm.at[pl.ds(mine, grp)], loc_sem.at[0])
-    w_l = pltpu.make_async_copy(lsest.at[0], lse_hbm.at[core], loc_sem.at[1])
-    w_o.start()
-    w_l.start()
-    x_o = push(ost.at[grp:2 * grp], o_hbm.at[pl.ds(mine, grp)], pair_send.at[4], pair_recv.at[4], to_partner)
-    x_l = push(lsest.at[1], lse_hbm.at[core], pair_send.at[5], pair_recv.at[5], to_partner)
-    dq_t = dot(kaug[:, :, 0:hd].reshape(NBLK * keys, hd), dsbuf[...].reshape(NBLK * keys, rows), TN)
-    dqst[...] = (jnp.transpose(dq_t) * scale).astype(jnp.bfloat16).reshape(2 * grp, tok, hd)
-    w_q = pltpu.make_async_copy(dqst.at[0:grp], dq_hbm.at[pl.ds(mine, grp)], loc_sem.at[2])
-    w_q.start()
-    x_dq = push(dqst.at[grp:2 * grp], dq_hbm.at[pl.ds(mine, grp)], pair_send.at[6], pair_recv.at[6], to_partner)
-
-    for a in (1, 3):
+        with scope('relay_b%d' % a):
+            for X in range(2):
+                relay_b(X, a)
+    with scope('bwd00'):
+        backward((0, 0))
+    with scope('relay_a2'):
         for o in range(CORES):
             for X in range(2):
-                relay_a(X, a, o)
+                relay_a(X, 2, o)
+
+    scope_out = scope('out_o')
+    scope_out.__enter__()
+    o_rows = jnp.transpose(o_t[...]).astype(jnp.bfloat16).reshape(2 * grp, tok, hd)
+    o_out[pl.ds(mine, grp)] = o_rows[0:grp]
+    ost[...] = o_rows[grp:2 * grp]
+    for h in range(grp):
+        lse_out[core, h:h + 1, :] = lse[:, h * tok:(h + 1) * tok]
+        lsest[h:h + 1, :] = lse[:, (grp + h) * tok:(grp + h + 1) * tok]
+    x_o = push(ost, o_out.at[pl.ds(mine, grp)], pair_send.at[4], pair_recv.at[4], to_partner)
+    x_l = push(lsest, lse_out.at[core], pair_send.at[5], pair_recv.at[5], to_partner)
+    scope_out.__exit__(None, None, None)
+    scope_out = scope('out_dq')
+    scope_out.__enter__()
+    dq_t = dot(kaug[:, :, 0:hd].reshape(NBLK * keys, hd), dsbuf[...].reshape(NBLK * keys, rows), TN)
+    dq_rows = (jnp.transpose(dq_t) * scale).astype(jnp.bfloat16).reshape(2 * grp, tok, hd)
+    dq_out[pl.ds(mine, grp)] = dq_rows[0:grp]
+    dqst[...] = dq_rows[grp:2 * grp]
+    x_dq = push(dqst, dq_out.at[pl.ds(mine, grp)], pair_send.at[6], pair_recv.at[6], to_partner)
+
+    scope_out.__exit__(None, None, None)
+    for a in (1, 3):
+        with scope('relay_a%d' % a):
+            for o in range(CORES):
+                for X in range(2):
+                    relay_a(X, a, o)
 
     def final(X, o):
         gather_b(X, 0, o)
@@ -373,26 +397,38 @@
         return total.astype(jnp.bfloat16)
 
     x_kv = []
-    for X in range(2):
-        kvsend[X] = final(X, 1)
-        x_kv.append(push(kvsend.at[X], kvrecv.at[X], pair_send.at[7 + X], pair_recv.at[7 + X], to_partner))
-    owns = [final(X, 0).astype(jnp.float32) for X in range(2)]
-    w_kv = []
-    for X, out in ((0, dk_hbm), (1, dv_hbm)):
+    with scope('final1'):
+        for X in range(2):
+            kvsend[X] = final(X, 1)
+            x_kv.append(push(kvsend.at[X], kvrecv.at[X], pair_send.at[7 + X], pair_recv.at[7 + X], to_partner))
+    with scope('final0'):
+        owns = [final(X, 0).astype(jnp.float32) for X in range(2)]
+    scope_out = scope('tail')
+    scope_out.__enter__()
+    for X, out in ((0, dk_out), (1, dv_out)):
         x_kv[X].wait_recv()
         got = kvrecv[X].astype(jnp.float32)
         tmp32[X, pl.ds(0, tok, stride=2), :] = jnp.where(core == 0, owns[X], got)
         tmp32[X, pl.ds(1, tok, stride=2), :] = jnp.where(core == 0, got, owns[X])
-        outb[X] = tmp32[X].astype(jnp.bfloat16)
-        w = pltpu.make_async_copy(outb.at[X], out, loc_sem.at[3 + X])
-        w.start()
-        w_kv.append(w)
+        out[...] = tmp32[X].astype(jnp.bfloat16)
     for c in sends:
         c.wait_send()
     for x in (x_o, x_l, x_dq):
         x.wait_recv()
-    for w in [w_o, w_l, w_q] + w_kv:
-        w.wait()
+    scope_out.__exit__(None, None, None)
+
+
+def store_kernel(o_in, lse_in, dq_in, dk_in, dv_in, o_out, lse_out, dq_out, dk_out, dv_out, lse_v, sem):
+    copies = [pltpu.make_async_copy(a, b, sem.at[i]) for i, (a, b) in enumerate(
+        ((o_in, o_out), (dq_in, dq_out), (dk_in, dk_out), (dv_in, dv_out), (lse_v, lse_out)))]
+    for c in copies[:4]:
+        c.start()
+    grp = lse_in.shape[1]
+    for i in range(lse_in.shape[0]):
+        lse_v[i * grp:(i + 1) * grp, :] = lse_in[i]
+    copies[4].start()
+    for c in copies:
+        c.wait()
 
 
 def solution(mesh):
@@ -408,7 +444,8 @@
         keys = CORES * tok
         assert kvh == CORES and cp == CORES * SIDE * SIDE and keys == hd
         bf, f32 = jnp.bfloat16, jnp.float32
-        any_spec = pl.BlockSpec(memory_space=pl.ANY)
+        hbm_spec = pl.BlockSpec(memory_space=pltpu.HBM)
+        vmem_spec = pl.BlockSpec(memory_space=pltpu.VMEM)
         n_rs = len(RKEYS)
         flat = lambda x: x.reshape(tok * kvh, hd)
         o, lse, dq, dk, dv = pl.pallas_call(
@@ -421,8 +458,8 @@
                 jax.ShapeDtypeStruct((tok * kvh, hd), bf),
                 jax.ShapeDtypeStruct((tok * kvh, hd), bf),
             ],
-            in_specs=[any_spec] * 6,
-            out_specs=[any_spec] * 5,
+            in_specs=[hbm_spec] * 6,
+            out_specs=[vmem_spec] * 5,
             scratch_shapes=[
                 pltpu.VMEM((2, tok * kvh, hd), bf),
                 pltpu.VMEM((2, tok * kvh, hd), f32),
@@ -438,13 +475,12 @@
                 pltpu.VMEM((NBLK, keys, rows), bf),
                 pltpu.VMEM((2, NBLK, CORES, tok, hd), f32),
                 pltpu.VMEM((2, n_rs, tok, hd), f32),
-                pltpu.VMEM((CORES * grp, tok, hd), bf),
-                pltpu.VMEM((CORES * grp, tok, hd), bf),
-                pltpu.VMEM((CORES, grp, tok), f32),
+                pltpu.VMEM((grp, tok, hd), bf),
+                pltpu.VMEM((grp, tok, hd), bf),
+                pltpu.VMEM((grp, tok), f32),
                 pltpu.VMEM((2, tok, hd), bf),
                 pltpu.VMEM((2, tok, hd), bf),
                 pltpu.VMEM((2, tok * kvh, hd), f32),
-                pltpu.VMEM((2, tok * kvh, hd), bf),
                 pltpu.VMEM((1, rows), f32),
                 pltpu.VMEM((1, rows), f32),
                 pltpu.VMEM((hd, rows), f32),
@@ -459,10 +495,25 @@
                 pltpu.SemaphoreType.DMA((2, n_rs)),
             ],
             compiler_params=pltpu.CompilerParams(
-                collective_id=0, has_side_effects=True, vmem_limit_bytes=60 * 1024 * 1024),
-        )(q.transpose(1, 0, 2), flat(k), flat(v), do.transpose(1, 0, 2), valid.reshape(1, tok), cu.reshape(1, n_docs + 1))
+                collective_id=0, has_side_effects=True, vmem_limit_bytes=40 * 1024 * 1024),
+        )(*(pltpu.with_memory_space_constraint(a, pltpu.HBM) for a in (q.transpose(1, 0, 2), flat(k), flat(v), do.transpose(1, 0, 2), valid.reshape(1, tok), cu.reshape(1, n_docs + 1))))
+        o, lse, dq, dk, dv = pl.pallas_call(
+            store_kernel,
+            name='store_outputs',
+            out_shape=[
+                jax.ShapeDtypeStruct((heads, tok, hd), bf),
+                jax.ShapeDtypeStruct((heads, tok), f32),
+                jax.ShapeDtypeStruct((heads, tok, hd), bf),
+                jax.ShapeDtypeStruct((tok * kvh, hd), bf),
+                jax.ShapeDtypeStruct((tok * kvh, hd), bf),
+            ],
+            in_specs=[vmem_spec] * 5,
+            out_specs=[hbm_spec] * 5,
+            scratch_shapes=[pltpu.VMEM((heads, tok), f32), pltpu.SemaphoreType.DMA((5,))],
+            compiler_params=pltpu.CompilerParams(vmem_limit_bytes=1024 * 1024),
+        )(o, lse, dq, dk, dv)
         back = lambda x: x.reshape(tok, kvh, hd)
-        return (o.transpose(1, 0, 2), lse.reshape(heads, tok).transpose(1, 0), dq.transpose(1, 0, 2), back(dk), back(dv))
+        return (o.transpose(1, 0, 2), lse.transpose(1, 0), dq.transpose(1, 0, 2), back(dk), back(dv))
 
     return jax.shard_map(
         local, mesh=mesh,

time: 48.1 us -> 43.2 us (0.90)
  local copies, waits for them, and re-layouts: 5.09 us -> 0 us
    unnamed x12 -> x0, local copies, waits for them, and re-layouts: 4.49 us -> none
    pallas_call x0 -> x1, Pallas kernels: none -> 0.8 us  [local(): pl.pallas_call(store_kernel, name='store_outputs', out_shape=[jax.ShapeDt...]
    reshape x1 -> x0, local copies, waits for them, and re-layouts: 0.6 us -> none  [local(): lse.reshape(heads, tok).transpose(1, 0)]
where the time goes in v2:
time: 43.2 us; the launch traced here: 43.1 us
  Pallas kernels  42.5 us (98%)
  between operations  0.64 us (1%)
    pallas_call x1, Pallas kernels, local(): pl.pallas_call(functools.partial(kernel, cp, n_docs, hd ** (-0.5)), name=...  41.7 us

profile of v2, /device:TPU:97, one launch (start us, length us, event | category | flops | bytes accessed | tf_op | source)
XLA Modules:
  0.0 43.1 jit_solution(5392567294278472480)
XLA Ops:
  0.6 41.7 %ring_attention.1 = (bf16[12,64,128]{2,1,0:T(8,128)(2,1)S(1)}, f32[2,6,64]{2,1,0:T(8,128)S(1)}, bf16[12,64,128]{2,1,0:T(8,128)(2,1)S(1)}, bf16[128,128]{1,0:T(8,128)(2,1)S(1)}, bf16[128,128]{1,0:T(8,128)(2,1)S(1)}) custom-call(bf16[12,64,128]{2,1,0:T(8,128)(2,1)} %bitcast.11, bf16[128,128]{1,0:T(8,128)(2,1)} %bitcast.13, bf16[128,128]{1,0:T(8,128)(2,1)} %bitcast.14, ...), custom_call_target="tpu_custom_call" | custom-call | tf_op jit(solution)/shard_map/ring_attention/pallas_call | solution.py:451
  42.3 0.8 %store_outputs.1 = (bf16[12,64,128]{2,1,0:T(8,128)(2,1)}, f32[12,64]{1,0:T(8,128)}, bf16[12,64,128]{2,1,0:T(8,128)(2,1)}, bf16[128,128]{1,0:T(8,128)(2,1)}, bf16[128,128]{1,0:T(8,128)(2,1)}) custom-call(bf16[12,64,128]{2,1,0:T(8,128)(2,1)S(1)} %get-tuple-element.15.o_in, f32[2,6,64]{2,1,0:T(8,128)S(1)} %get-tuple-element.16.lse_in, ...), custom_call_target="tpu_custom_call" | custom-call | tf_op jit(solution)/shard_map/store_outputs/pallas_call | solution.py:500

commit v3 on v2

--- a/solution.py
+++ b/solution.py
@@ -13,16 +13,48 @@
 NEG = -(2.0 ** 126)
 CORES = 2
 SIDE = 4
-LEVELS = (
+GROUPS = (
     ((0, 0),),
     ((1, 0), (3, 0), (0, 1), (0, 3)),
-    ((2, 0), (0, 2), (1, 1), (1, 3), (3, 1), (3, 3)),
+    ((1, 1), (1, 3), (3, 1), (3, 3)),
+    ((2, 0), (0, 2)),
     ((2, 1), (2, 3), (1, 2), (3, 2)),
     ((2, 2),),
 )
-BLOCKS = tuple(blk for level in LEVELS for blk in level)
+BLOCKS = tuple(blk for group in GROUPS for blk in group)
 SLOT = {blk: i for i, blk in enumerate(BLOCKS)}
 NBLK = len(BLOCKS)
+GATHER = (
+    (0, 0, 0, 0, 0, 2), (0, 0, 0, 0, 0, 1), (1, 0, 0, 0, 0, 1), (1, 0, 0, 0, 0, 2), (1, 0, 0, 0, 0, -1),
+    (0, 0, 0, 0, 0, -1), (0, 0, 0, 1, 0, -1), (0, 0, 0, 1, 0, 2), (1, 0, 0, 1, 1, 2), (1, 0, 0, 1, 0, 2),
+    (0, 0, 0, 0, 1, 2), (0, 0, 0, 1, 0, 1), (1, 0, 0, 1, 0, -1), (1, 0, 0, 0, 1, 2), (0, 0, 0, 1, 1, 1),
+    (1, 0, 0, 1, 1, 1), (1, 0, 0, 0, 1, -1), (1, 0, 0, 1, 1, -1), (1, 0, 0, 0, 1, 1), (1, 0, 0, 1, 0, 1),
+    (0, 0, 0, 1, 1, -1), (0, 0, 0, 0, 1, -1), (0, 0, 0, 0, 1, 1), (0, 1, 0, 0, 1, 2), (1, 1, 0, 0, 1, 2),
+    (0, 2, 0, 0, 1, -1), (0, 0, 0, 1, 1, 2), (1, 2, 0, 0, 1, 2), (0, 2, 0, 0, 1, 2), (1, 2, 0, 0, 1, 1),
+    (0, 2), (1, 2, 0, 0, 1, -1), (0, 1, 0, 0, 1, -1), (0, 3, 0, 0, 1, 2), (1, 1, 0, 1, 1, 2),
+    (0, 1, 0, 1, 1, 2), (1, 2, 0, 1, 1, 2), (0, 2, 0, 1, 1, 2), (1, 2, 0, 1, 1, 1), (0, 0),
+    (1, 2, 0, 1, 1, -1), (3, 2), (0, 3, 0, 1, 1, 2), (1, 3, 0, 1, 1, 2), (1, 3, 0, 0, 1, 2),
+    (0, 2, 0, 0, 1, 1), (0, 2, 0, 1, 1, -1), (1, 2), (1, 3, 0, 1, 1, 1), (0, 2, 0, 1, 1, 1),
+    (1, 0), (0, 1, 0, 1, 1, -1), (0, 1), (1, 3, 0, 1, 1, -1), (1, 3, 0, 0, 1, 1),
+    (0, 1, 0, 0, 1, 1), (0, 3, 0, 1, 1, -1), (1, 3, 0, 0, 1, -1), (1, 1, 0, 1, 1, -1), (1, 1),
+    (0, 3, 0, 0, 1, 1), (0, 3, 0, 1, 1, 1), (0, 1, 0, 1, 1, 1), (0, 3, 0, 0, 1, -1), (1, 1, 0, 0, 1, -1),
+    (1, 1, 0, 1, 1, 1), (1, 1, 0, 0, 1, 1), (3, 0), (3, 1), (5, 2),
+    (5, 0), (5, 1), (4, 2), (4, 0), (4, 1),
+    (2, 0), (2, 1),
+)
+SCATTER = (
+    (2, 1), (0, 2, 1, 0), (1, 1, 2, 0), (2, 2), (0, 2, 2, 0), (1, 2, 2, 1), (0, 2, 2, 1), (3, 2),
+    (0, 3, 2, 1), (0, 3, 2, 0), (1, 1, 2, 1), (1, 2, 3, 1), (1, 2), (0, 2), (1, 2, 2, 0), (0, 1, 2, 0),
+    (2, 3), (2, 0), (1, 3, 2, 1), (0, 0, 2, 1), (0, 0, 2, 0), (1, 0, 2, 0), (0, 1, 2, 1), (1, 0, 2, 1),
+    (2, 2, -1), (1, 3), (1, 3, 2, 0), (0, 0), (0, 1, 3, 1), (1, 3, 1, 0), (3, 3), (1, 1),
+    (0, 3, 3, 1), (3, 1), (0, 3, 1, 0), (1, 1, 1, 0), (1, 3, 3, 1), (1, 1, 3, 1), (0, 2, 3, 1), (0, 2, 3, 0),
+    (1, 1, 1, 1), (0, 2, 1, 1), (0, 3, 1, 1), (0, 1), (3, 0), (0, 3), (1, 2, 3, 0), (0, 1, 3, 0),
+    (1, 2, 1, 1), (1, 3, 1, 1), (1, 1, 3, 0), (0, 0, 3, 0), (0, 1, 1, 1), (1, 0), (0, 0, 1, 1), (0, 1, 1, 0),
+    (1, 2, 1, 0), (1, 0, 3, 1), (1, 3, 3, 0), (0, 3, 3, 0), (1, 0, 1, 1), (0, 3, 0, 1), (1,), (1, 1, 0, 1),
+    (0, 2, 0, 1), (1, 2, 0, 1), (0, 0, 1, 0), (0, 2, 0, 0), (0, 0, 3, 1), (1, 0, 3, 0), (0, 1, 0, 1), (1, 0, 1, 0),
+    (1, 3, 0, 1), (0, 1, 0, 0), (1, 2, 0, 0), (1, 1, 0, 0), (1, 3, 0, 0), (0,), (0, 3, 0, 0), (0, 0, 0, 1),
+    (1, 0, 0, 1), (1, 0, 0, 0), (0, 0, 0, 0),
+)
 NT = (((1,), (1,)), ((), ()))
 TN = (((0,), (0,)), ((), ()))
 
@@ -39,36 +71,40 @@
     return (a, b) if X == 0 else (b, a)
 
 
-def routes(X, blk, o):
-    a, b = frame(X, blk)
-    out = []
-    if b == 0:
-        if a == 3 and o == 0:
-            out.append((1, 0))
-        if a == 1 and o == 1:
-            out.append((-1, 0))
-        if a == 0:
-            out += [(1, 0), (-1, 0)]
-        out += [(0, 1), (0, -1)]
-    elif b == 3 and o == 0:
-        out.append((0, 1))
-    elif b == 1 and o == 1:
-        out.append((0, -1))
-    return [unframe(X, *step) for step in out]
-
-
-RKEYS = []
+def terms(a, b, o):
+    if b == 3:
+        return [('rb', a, o)] if o == 0 else []
+    if b == 1:
+        return [('rb', a, o)] if o == 1 else []
+    if b == 2:
+        return []
+    out = [('fb', a, o, 1), ('fb', a, o, -1)]
+    if a == 0:
+        out += [('fa', o, 1), ('fa', o, -1), ('ra', o)]
+    return out
+
+
+def target(a, b, o):
+    if b == 2:
+        return (0, -1 if o == 0 else 1), ('rb', a, o)
+    if b:
+        return (0, -1 if b == 3 else 1), ('fb', a, o, 1 if b == 3 else -1)
+    if a == 2:
+        return (2, 0), ('ra', o)
+    return (-1 if a == 3 else 1, 0), ('fa', o, 1 if a == 3 else -1)
+
+
+RIDX = {}
 for _a in range(SIDE):
-    RKEYS += [('rb', _a, 0), ('rb', _a, 1)]
-    RKEYS += [('fb', _a, _o, _s) for _o in range(2) for _s in (1, -1)]
-RKEYS += [('ra', 0), ('ra', 1)]
-RKEYS += [('fa', _o, _s) for _o in range(2) for _s in (1, -1)]
-RIDX = {key: i for i, key in enumerate(RKEYS)}
+    for _b in range(SIDE):
+        for _o in range(CORES):
+            if (_a, _b) != (0, 0):
+                RIDX[target(_a, _b, _o)[1]] = len(RIDX)
 
 
 def kernel(cp, n_docs, scale, q_hbm, k_hbm, v_hbm, do_hbm, val_hbm, cu_hbm,
            o_out, lse_out, dq_out, dk_out, dv_out,
-           kin, kf32, oth, kv, kaug, qaug, dob, dot_t, sbuf, dpbuf, pbuf, dsbuf, part, rbuf,
+           kin, kf32, oth, kv, kaug, qbuf, qt, dob, dot_t, dot_b, sbuf, dpbuf, pbuf, dsbuf, part, rbuf,
            ost, dqst, lsest, kvsend, kvrecv, tmp32, m_ref, l_ref, o_t, valv, cus,
            loc_sem, pair_send, pair_recv, ag_send, ag_recv, rs_send, rs_recv):
     tok = valv.shape[1]
@@ -97,13 +133,13 @@
     c_v = pltpu.make_async_copy(v_hbm, kin.at[1], loc_sem.at[1])
     c_val = pltpu.make_async_copy(val_hbm, valv, loc_sem.at[2])
     c_cu = pltpu.make_async_copy(cu_hbm, cus, loc_sem.at[3])
-    c_q = pltpu.make_async_copy(q_hbm.at[pl.ds(mine, grp)], qaug.at[0:grp, :, 0:hd], loc_sem.at[4])
+    c_q = pltpu.make_async_copy(q_hbm.at[pl.ds(mine, grp)], qbuf.at[0:grp], loc_sem.at[4])
     c_do = pltpu.make_async_copy(do_hbm.at[pl.ds(mine, grp)], dob.at[0:grp], loc_sem.at[5])
     for c in (c_k, c_v, c_val, c_cu, c_q, c_do):
         c.start()
 
     barrier = pltpu.get_barrier_semaphore()
-    peers = [to_partner] + [nbr(s) for s in ((1, 0), (-1, 0), (0, 1), (0, -1))]
+    peers = [to_partner] + [nbr(s) for s in ((1, 0), (-1, 0), (2, 0), (0, 1), (0, -1), (0, 2))]
     for peer in peers:
         pl.semaphore_signal(barrier, inc=1, device_id=peer, device_id_type=MESH)
 
@@ -144,32 +180,37 @@
     with scope('barrier'):
         pl.semaphore_wait(barrier, len(peers))
 
+    here = {(X, (0, 0), 0) for X in range(2)}
     ag_count = [0]
 
-    def forward(X, blk, o):
-        for step in routes(X, blk, o):
-            dst_blk = ((blk[0] - step[0]) % SIDE, (blk[1] - step[1]) % SIDE)
-            s = SLOT[dst_blk]
-            push(kv.at[X, SLOT[blk], o], kv.at[X, s, o], ag_send.at[ag_count[0]], ag_recv.at[X, s, o], nbr(step))
-            ag_count[0] += 1
-
     def arrive(X, blk, o):
-        s = SLOT[blk]
-        remote(kv.at[X, s, o], kv.at[X, s, o], ag_send.at[0], ag_recv.at[X, s, o], to_partner).wait_recv()
+        if (X, blk, o) not in here:
+            s = SLOT[blk]
+            remote(kv.at[X, s, o], kv.at[X, s, o], ag_send.at[0], ag_recv.at[X, s, o], to_partner).wait_recv()
+            here.add((X, blk, o))
+
+    def forward(X, a, b, o, phase, step):
+        blk = unframe(X, a, b)
+        arrive(X, blk, o)
+        step = unframe(X, step * (1 - phase), step * phase)
+        d = SLOT[(blk[0] - step[0]) % SIDE, (blk[1] - step[1]) % SIDE]
+        push(kv.at[X, SLOT[blk], o], kv.at[X, d, o], ag_send.at[ag_count[0]], ag_recv.at[X, d, o], nbr(step))
+        ag_count[0] += 1
 
     for X in range(2):
         push(oth.at[X], kv.at[X, 0, 1], pair_send.at[X], ag_recv.at[X, 0, 1], to_partner)
-    for X in range(2):
-        forward(X, (0, 0), 0)
-    x_q = push(q_hbm.at[pl.ds(theirs, grp)], qaug.at[grp:2 * grp, :, 0:hd], pair_send.at[2], pair_recv.at[2], to_partner)
+    early = 0
+    while len(GATHER[early]) == 6 and GATHER[early][1:4] == (0, 0, 0):
+        forward(*GATHER[early])
+        early += 1
+    x_q = push(q_hbm.at[pl.ds(theirs, grp)], qbuf.at[grp:2 * grp], pair_send.at[2], pair_recv.at[2], to_partner)
     x_do = push(do_hbm.at[pl.ds(theirs, grp)], dob.at[grp:2 * grp], pair_send.at[3], pair_recv.at[3], to_partner)
 
     t_row = lax.broadcasted_iota(jnp.int32, (tok, hd), 0)
-    t_lane = lax.broadcasted_iota(jnp.int32, (tok, hd), 1)
-    for o in range(CORES):
-        hot = jnp.where(t_lane == t_row + o * tok, 1.0, 0.0).astype(jnp.bfloat16)
-        for h in range(grp):
-            qaug[o * grp + h, :, hd:2 * hd] = hot
+    t_sub = lax.broadcasted_iota(jnp.int32, (keys, rows), 0)
+    t_lane = lax.broadcasted_iota(jnp.int32, (keys, rows), 1)
+    token = lax.rem(t_lane, tok) + jnp.where(t_lane >= grp * tok, tok, 0)
+    qt[hd:hd + keys, :] = jnp.where(t_sub == token, 1.0, 0.0).astype(jnp.bfloat16)
 
     with scope('wait_cu'):
         c_cu.wait()
@@ -211,20 +252,20 @@
 
     c2 = scale * math.log2(math.e)
 
-    def scores(level):
-        lo, n = SLOT[level[0]], len(level)
-        for blk in level:
+    def scores(group):
+        lo, n = SLOT[group[0]], len(group)
+        for blk in group:
             prepare(blk)
-        ka = kaug[lo:lo + n].reshape(n * keys, 2 * hd)
-        sbuf[lo:lo + n] = dot(ka, qaug[...].reshape(rows, 2 * hd), NT).reshape(n, keys, rows)
-
-    def grads_p(level):
-        lo, n = SLOT[level[0]], len(level)
+        s = dot(kaug[lo:lo + n].reshape(n * keys, 2 * hd), qt[...])
+        sbuf[lo:lo + n] = s.reshape(n, keys, rows)
+
+    def grads_p(group):
+        lo, n = SLOT[group[0]], len(group)
         vb = kv[1, lo:lo + n].reshape(n * keys, hd)
-        dpbuf[lo:lo + n] = dot(vb, dob[...].reshape(rows, hd), NT).reshape(n, keys, rows)
-
-    def softmax(level, first):
-        lo, n = SLOT[level[0]], len(level)
+        dpbuf[lo:lo + n] = dot(vb, dot_b[...]).reshape(n, keys, rows)
+
+    def softmax(group, first):
+        lo, n = SLOT[group[0]], len(group)
         mx = jnp.max(sbuf[lo:lo + n].reshape(n * keys, rows), axis=0, keepdims=True)
         if first:
             m_new = mx
@@ -248,37 +289,38 @@
             l_ref[...] = l_ref[...] * alpha + total
             o_t[...] = o_t[...] * alpha + pv
 
-    with scope('pair_kv'):
-        for X in range(2):
-            arrive(X, (0, 0), 1)
-            forward(X, (0, 0), 1)
-    with scope('pair_q'):
-        c_q.wait()
-        x_q.wait_recv()
-    with scope('scores0'):
-        scores(LEVELS[0])
-    with scope('pair_do'):
-        c_do.wait()
-        x_do.wait_recv()
-    with scope('do_t'):
-        dot_t[...] = jnp.transpose(dob[...].reshape(rows, hd).astype(jnp.float32))
-    with scope('softmax0'):
-        softmax(LEVELS[0], True)
-    with scope('grads_p0'):
-        grads_p(LEVELS[0])
-    for i, level in enumerate(LEVELS[1:], 1):
-        with scope('gather%d' % i):
-            for o in range(CORES):
-                for blk in level:
-                    for X in range(2):
-                        arrive(X, blk, o)
-                        forward(X, blk, o)
-        with scope('scores%d' % i):
-            scores(level)
-        with scope('softmax%d' % i):
-            softmax(level, False)
-        with scope('grads_p%d' % i):
-            grads_p(level)
+    started = [False, False, False]
+    for item in GATHER[early:]:
+        if len(item) == 6:
+            with scope('fwd%d_%d%d_%d' % item[:4]):
+                forward(*item)
+            continue
+        gi, stage = item
+        group = GROUPS[gi]
+        with scope('wait%d_%d' % item):
+            for blk in group:
+                for o in range(CORES):
+                    arrive(min(stage, 1), blk, o)
+            if not started[0]:
+                c_q.wait()
+                x_q.wait_recv()
+                qt[0:hd, :] = jnp.transpose(qbuf[...].reshape(rows, hd).astype(jnp.float32)).astype(jnp.bfloat16)
+                started[0] = True
+            if stage == 2 and not started[1]:
+                c_do.wait()
+                x_do.wait_recv()
+                do_t = jnp.transpose(dob[...].reshape(rows, hd).astype(jnp.float32))
+                dot_t[...] = do_t
+                dot_b[...] = do_t.astype(jnp.bfloat16)
+                started[1] = True
+        with scope('group%d_%d' % item):
+            if stage == 0:
+                scores(group)
+            elif stage == 1:
+                softmax(group, not started[2])
+                started[2] = True
+            else:
+                grads_p(group)
 
     scope_fin = scope('finish')
     scope_fin.__enter__()
@@ -302,35 +344,14 @@
         remote(rbuf.at[X, i], rbuf.at[X, i], rs_send.at[X, i], rs_recv.at[X, i], to_partner).wait_recv()
         return rbuf[X, i]
 
-    def immediate(X, blk):
-        a, b = frame(X, blk)
-        if b == 2:
-            rsend(X, blk, 0, ('rb', a, 0), (0, -1))
-            rsend(X, blk, 1, ('rb', a, 1), (0, 1))
-        elif b == 3:
-            rsend(X, blk, 1, ('fb', a, 1, 1), (0, -1))
-        elif b == 1:
-            rsend(X, blk, 0, ('fb', a, 0, -1), (0, 1))
-
-    def relay_b(X, a):
-        for b, o, step, sgn in ((3, 0, -1, 1), (1, 1, 1, -1)):
-            blk = unframe(X, a, b)
-            part[X, SLOT[blk], o] += rwait(X, ('rb', a, o))
-            rsend(X, blk, o, ('fb', a, o, sgn), (0, step))
-
-    def gather_b(X, a, o):
-        blk = unframe(X, a, 0)
-        part[X, SLOT[blk], o] += rwait(X, ('fb', a, o, 1)) + rwait(X, ('fb', a, o, -1))
-        return blk
-
-    def relay_a(X, a, o):
-        blk = gather_b(X, a, o)
-        if a == 2:
-            rsend(X, blk, o, ('ra', o), (-1 if o == 0 else 1, 0))
-        else:
-            if (a == 3) == (o == 0):
-                part[X, SLOT[blk], o] += rwait(X, ('ra', o))
-            rsend(X, blk, o, ('fa', o, 1 if a == 3 else -1), (-1 if a == 3 else 1, 0))
+    def total(X, a, b, o):
+        s = SLOT[unframe(X, a, b)]
+        keys_in = terms(a, b, o)
+        if keys_in:
+            acc = part[X, s, o]
+            for key in keys_in:
+                acc = acc + rwait(X, key)
+            part[X, s, o] = acc
 
     def backward(blk):
         s = SLOT[blk]
@@ -338,71 +359,58 @@
         pbuf[s] = p.astype(jnp.bfloat16)
         dsbuf[s] = (p * (dpbuf[s] - delta)).astype(jnp.bfloat16)
         part[1, s] = dot(pbuf[s], dob[...].reshape(rows, hd)).reshape(CORES, tok, hd)
-        part[0, s] = dot(dsbuf[s], qaug[:, :, 0:hd].reshape(rows, hd)).reshape(CORES, tok, hd)
-        for X in range(2):
-            immediate(X, blk)
-
-    for level in (LEVELS[4], LEVELS[3], LEVELS[2]):
-        for blk in level:
-            with scope('bwd%d%d' % blk):
-                backward(blk)
-    with scope('relay_b2'):
-        for X in range(2):
-            relay_b(X, 2)
-    for blk in LEVELS[1]:
-        with scope('bwd%d%d' % blk):
-            backward(blk)
-    for a in (1, 3, 0):
-        with scope('relay_b%d' % a):
-            for X in range(2):
-                relay_b(X, a)
-    with scope('bwd00'):
-        backward((0, 0))
-    with scope('relay_a2'):
-        for o in range(CORES):
-            for X in range(2):
-                relay_a(X, 2, o)
-
-    scope_out = scope('out_o')
-    scope_out.__enter__()
-    o_rows = jnp.transpose(o_t[...]).astype(jnp.bfloat16).reshape(2 * grp, tok, hd)
-    o_out[pl.ds(mine, grp)] = o_rows[0:grp]
-    ost[...] = o_rows[grp:2 * grp]
-    for h in range(grp):
-        lse_out[core, h:h + 1, :] = lse[:, h * tok:(h + 1) * tok]
-        lsest[h:h + 1, :] = lse[:, (grp + h) * tok:(grp + h + 1) * tok]
-    x_o = push(ost, o_out.at[pl.ds(mine, grp)], pair_send.at[4], pair_recv.at[4], to_partner)
-    x_l = push(lsest, lse_out.at[core], pair_send.at[5], pair_recv.at[5], to_partner)
-    scope_out.__exit__(None, None, None)
-    scope_out = scope('out_dq')
-    scope_out.__enter__()
-    dq_t = dot(kaug[:, :, 0:hd].reshape(NBLK * keys, hd), dsbuf[...].reshape(NBLK * keys, rows), TN)
-    dq_rows = (jnp.transpose(dq_t) * scale).astype(jnp.bfloat16).reshape(2 * grp, tok, hd)
-    dq_out[pl.ds(mine, grp)] = dq_rows[0:grp]
-    dqst[...] = dq_rows[grp:2 * grp]
-    x_dq = push(dqst, dq_out.at[pl.ds(mine, grp)], pair_send.at[6], pair_recv.at[6], to_partner)
-
-    scope_out.__exit__(None, None, None)
-    for a in (1, 3):
-        with scope('relay_a%d' % a):
-            for o in range(CORES):
-                for X in range(2):
-                    relay_a(X, a, o)
-
-    def final(X, o):
-        gather_b(X, 0, o)
-        total = part[X, 0, o] + rwait(X, ('fa', o, 1)) + rwait(X, ('fa', o, -1))
-        if X == 0:
-            total = total * scale
-        return total.astype(jnp.bfloat16)
-
-    x_kv = []
-    with scope('final1'):
-        for X in range(2):
-            kvsend[X] = final(X, 1)
-            x_kv.append(push(kvsend.at[X], kvrecv.at[X], pair_send.at[7 + X], pair_recv.at[7 + X], to_partner))
-    with scope('final0'):
-        owns = [final(X, 0).astype(jnp.float32) for X in range(2)]
+        part[0, s] = dot(dsbuf[s], qbuf[...].reshape(rows, hd)).reshape(CORES, tok, hd)
+
+    x_out = []
+
+    def store_o():
+        o_rows = jnp.transpose(o_t[...]).astype(jnp.bfloat16).reshape(2 * grp, tok, hd)
+        o_out[pl.ds(mine, grp)] = o_rows[0:grp]
+        ost[...] = o_rows[grp:2 * grp]
+        for h in range(grp):
+            lse_out[core, h:h + 1, :] = lse[:, h * tok:(h + 1) * tok]
+            lsest[h:h + 1, :] = lse[:, (grp + h) * tok:(grp + h + 1) * tok]
+        x_out.append(push(ost, o_out.at[pl.ds(mine, grp)], pair_send.at[4], pair_recv.at[4], to_partner))
+        x_out.append(push(lsest, lse_out.at[core], pair_send.at[5], pair_recv.at[5], to_partner))
+
+    def store_dq():
+        dq_t = dot(kaug[:, :, 0:hd].reshape(NBLK * keys, hd), dsbuf[...].reshape(NBLK * keys, rows), TN)
+        dq_rows = (jnp.transpose(dq_t) * scale).astype(jnp.bfloat16).reshape(2 * grp, tok, hd)
+        dq_out[pl.ds(mine, grp)] = dq_rows[0:grp]
+        dqst[...] = dq_rows[grp:2 * grp]
+        x_out.append(push(dqst, dq_out.at[pl.ds(mine, grp)], pair_send.at[6], pair_recv.at[6], to_partner))
+
+    x_kv, owns = {}, {}
+
+    def finish(X, o):
+        total(X, 0, 0, o)
+        res = part[X, 0, o] * scale if X == 0 else part[X, 0, o]
+        if o == 1:
+            kvsend[X] = res.astype(jnp.bfloat16)
+            x_kv[X] = push(kvsend.at[X], kvrecv.at[X], pair_send.at[7 + X], pair_recv.at[7 + X], to_partner)
+        else:
+            owns[X] = res.astype(jnp.bfloat16).astype(jnp.float32)
+
+    for item in SCATTER:
+        if len(item) == 3:
+            with scope('late%d_%d' % item[:2]):
+                grads_p(GROUPS[item[0]])
+        elif len(item) == 2:
+            with scope('bwd%d%d' % item):
+                backward(item)
+        elif len(item) == 1:
+            with scope('store%d' % item):
+                (store_o, store_dq)[item[0]]()
+        elif item[1:3] == (0, 0):
+            with scope('final%d_%d' % (item[0], item[3])):
+                finish(item[0], item[3])
+        else:
+            X, a, b, o = item
+            with scope('sum%d_%d%d_%d' % item):
+                total(X, a, b, o)
+                step, key = target(a, b, o)
+                rsend(X, unframe(X, a, b), o, key, step)
+
     scope_out = scope('tail')
     scope_out.__enter__()
     for X, out in ((0, dk_out), (1, dv_out)):
@@ -413,7 +421,7 @@
         out[...] = tmp32[X].astype(jnp.bfloat16)
     for c in sends:
         c.wait_send()
-    for x in (x_o, x_l, x_dq):
+    for x in x_out:
         x.wait_recv()
     scope_out.__exit__(None, None, None)
 
@@ -446,7 +454,7 @@
         bf, f32 = jnp.bfloat16, jnp.float32
         hbm_spec = pl.BlockSpec(memory_space=pltpu.HBM)
         vmem_spec = pl.BlockSpec(memory_space=pltpu.VMEM)
-        n_rs = len(RKEYS)
+        n_rs = len(RIDX)
         flat = lambda x: x.reshape(tok * kvh, hd)
         o, lse, dq, dk, dv = pl.pallas_call(
             functools.partial(kernel, cp, n_docs, hd ** -0.5),
@@ -466,9 +474,11 @@
                 pltpu.VMEM((2, tok, hd), bf),
                 pltpu.VMEM((2, NBLK, CORES, tok, hd), bf),
                 pltpu.VMEM((NBLK, keys, 2 * hd), bf),
-                pltpu.VMEM((CORES * grp, tok, 2 * hd), bf),
+                pltpu.VMEM((CORES * grp, tok, hd), bf),
+                pltpu.VMEM((hd + keys, rows), bf),
                 pltpu.VMEM((CORES * grp, tok, hd), bf),
                 pltpu.VMEM((hd, rows), f32),
+                pltpu.VMEM((hd, rows), bf),
                 pltpu.VMEM((NBLK, keys, rows), f32),
                 pltpu.VMEM((NBLK, keys, rows), f32),
                 pltpu.VMEM((NBLK, keys, rows), bf),

time: 43.2 us -> 39 us (0.903)
  Pallas kernels: 42.5 us -> 38.3 us
    pallas_call x1, Pallas kernels: 41.7 us -> 37.5 us  [local(): pl.pallas_call(functools.partial(kernel, cp, n_docs, hd ** (-0.5)), name=...]
where the time goes in v3:
time: 39 us; the launch traced here: 38.9 us
  Pallas kernels  38.3 us (98%)
  between operations  0.64 us (2%)
    pallas_call x1, Pallas kernels, local(): pl.pallas_call(functools.partial(kernel, cp, n_docs, hd ** (-0.5)), name=...  37.5 us
    pallas_call x1, Pallas kernels, local(): pl.pallas_call(store_kernel, name='store_outputs', out_shape=[jax.ShapeDt...  0.8 us

profile of v3, /device:TPU:97, one launch (start us, length us, event | category | flops | bytes accessed | tf_op | source)
XLA Modules:
  0.0 38.9 jit_solution(6296189408942858153)
XLA Ops:
  0.6 37.5 %ring_attention.1 = (bf16[12,64,128]{2,1,0:T(8,128)(2,1)S(1)}, f32[2,6,64]{2,1,0:T(8,128)S(1)}, bf16[12,64,128]{2,1,0:T(8,128)(2,1)S(1)}, bf16[128,128]{1,0:T(8,128)(2,1)S(1)}, bf16[128,128]{1,0:T(8,128)(2,1)S(1)}) custom-call(bf16[12,64,128]{2,1,0:T(8,128)(2,1)} %bitcast.11, bf16[128,128]{1,0:T(8,128)(2,1)} %bitcast.13, bf16[128,128]{1,0:T(8,128)(2,1)} %bitcast.14, ...), custom_call_target="tpu_custom_call" | custom-call | tf_op jit(solution)/shard_map/ring_attention/pallas_call | solution.py:459
  38.1 0.8 %store_outputs.1 = (bf16[12,64,128]{2,1,0:T(8,128)(2,1)}, f32[12,64]{1,0:T(8,128)}, bf16[12,64,128]{2,1,0:T(8,128)(2,1)}, bf16[128,128]{1,0:T(8,128)(2,1)}, bf16[128,128]{1,0:T(8,128)(2,1)}) custom-call(bf16[12,64,128]{2,1,0:T(8,128)(2,1)S(1)} %get-tuple-element.15.o_in, f32[2,6,64]{2,1,0:T(8,128)S(1)} %get-tuple-element.16.lse_in, ...), custom_call_target="tpu_custom_call" | custom-call | tf_op jit(solution)/shard_map/store_outputs/pallas_call | solution.py:510

commit v4 on v3

--- a/solution.py
+++ b/solution.py
@@ -24,36 +24,40 @@
 BLOCKS = tuple(blk for group in GROUPS for blk in group)
 SLOT = {blk: i for i, blk in enumerate(BLOCKS)}
 NBLK = len(BLOCKS)
-GATHER = (
-    (0, 0, 0, 0, 0, 2), (0, 0, 0, 0, 0, 1), (1, 0, 0, 0, 0, 1), (1, 0, 0, 0, 0, 2), (1, 0, 0, 0, 0, -1),
-    (0, 0, 0, 0, 0, -1), (0, 0, 0, 1, 0, -1), (0, 0, 0, 1, 0, 2), (1, 0, 0, 1, 1, 2), (1, 0, 0, 1, 0, 2),
-    (0, 0, 0, 0, 1, 2), (0, 0, 0, 1, 0, 1), (1, 0, 0, 1, 0, -1), (1, 0, 0, 0, 1, 2), (0, 0, 0, 1, 1, 1),
-    (1, 0, 0, 1, 1, 1), (1, 0, 0, 0, 1, -1), (1, 0, 0, 1, 1, -1), (1, 0, 0, 0, 1, 1), (1, 0, 0, 1, 0, 1),
-    (0, 0, 0, 1, 1, -1), (0, 0, 0, 0, 1, -1), (0, 0, 0, 0, 1, 1), (0, 1, 0, 0, 1, 2), (1, 1, 0, 0, 1, 2),
-    (0, 2, 0, 0, 1, -1), (0, 0, 0, 1, 1, 2), (1, 2, 0, 0, 1, 2), (0, 2, 0, 0, 1, 2), (1, 2, 0, 0, 1, 1),
-    (0, 2), (1, 2, 0, 0, 1, -1), (0, 1, 0, 0, 1, -1), (0, 3, 0, 0, 1, 2), (1, 1, 0, 1, 1, 2),
-    (0, 1, 0, 1, 1, 2), (1, 2, 0, 1, 1, 2), (0, 2, 0, 1, 1, 2), (1, 2, 0, 1, 1, 1), (0, 0),
-    (1, 2, 0, 1, 1, -1), (3, 2), (0, 3, 0, 1, 1, 2), (1, 3, 0, 1, 1, 2), (1, 3, 0, 0, 1, 2),
-    (0, 2, 0, 0, 1, 1), (0, 2, 0, 1, 1, -1), (1, 2), (1, 3, 0, 1, 1, 1), (0, 2, 0, 1, 1, 1),
-    (1, 0), (0, 1, 0, 1, 1, -1), (0, 1), (1, 3, 0, 1, 1, -1), (1, 3, 0, 0, 1, 1),
-    (0, 1, 0, 0, 1, 1), (0, 3, 0, 1, 1, -1), (1, 3, 0, 0, 1, -1), (1, 1, 0, 1, 1, -1), (1, 1),
-    (0, 3, 0, 0, 1, 1), (0, 3, 0, 1, 1, 1), (0, 1, 0, 1, 1, 1), (0, 3, 0, 0, 1, -1), (1, 1, 0, 0, 1, -1),
-    (1, 1, 0, 1, 1, 1), (1, 1, 0, 0, 1, 1), (3, 0), (3, 1), (5, 2),
-    (5, 0), (5, 1), (4, 2), (4, 0), (4, 1),
-    (2, 0), (2, 1),
-)
-SCATTER = (
-    (2, 1), (0, 2, 1, 0), (1, 1, 2, 0), (2, 2), (0, 2, 2, 0), (1, 2, 2, 1), (0, 2, 2, 1), (3, 2),
-    (0, 3, 2, 1), (0, 3, 2, 0), (1, 1, 2, 1), (1, 2, 3, 1), (1, 2), (0, 2), (1, 2, 2, 0), (0, 1, 2, 0),
-    (2, 3), (2, 0), (1, 3, 2, 1), (0, 0, 2, 1), (0, 0, 2, 0), (1, 0, 2, 0), (0, 1, 2, 1), (1, 0, 2, 1),
-    (2, 2, -1), (1, 3), (1, 3, 2, 0), (0, 0), (0, 1, 3, 1), (1, 3, 1, 0), (3, 3), (1, 1),
-    (0, 3, 3, 1), (3, 1), (0, 3, 1, 0), (1, 1, 1, 0), (1, 3, 3, 1), (1, 1, 3, 1), (0, 2, 3, 1), (0, 2, 3, 0),
-    (1, 1, 1, 1), (0, 2, 1, 1), (0, 3, 1, 1), (0, 1), (3, 0), (0, 3), (1, 2, 3, 0), (0, 1, 3, 0),
-    (1, 2, 1, 1), (1, 3, 1, 1), (1, 1, 3, 0), (0, 0, 3, 0), (0, 1, 1, 1), (1, 0), (0, 0, 1, 1), (0, 1, 1, 0),
-    (1, 2, 1, 0), (1, 0, 3, 1), (1, 3, 3, 0), (0, 3, 3, 0), (1, 0, 1, 1), (0, 3, 0, 1), (1,), (1, 1, 0, 1),
-    (0, 2, 0, 1), (1, 2, 0, 1), (0, 0, 1, 0), (0, 2, 0, 0), (0, 0, 3, 1), (1, 0, 3, 0), (0, 1, 0, 1), (1, 0, 1, 0),
-    (1, 3, 0, 1), (0, 1, 0, 0), (1, 2, 0, 0), (1, 1, 0, 0), (1, 3, 0, 0), (0,), (0, 3, 0, 0), (0, 0, 0, 1),
-    (1, 0, 0, 1), (1, 0, 0, 0), (0, 0, 0, 0),
+ORDER = (
+    (0, 0, 0, 0, 1, 0, 2), (0, 1, 0, 0, 1, 0, 2), (0, 1, 0, 0, 0, 0, 2), (0, 0, 0, 0, 1, 0, 1), (0, 0, 0, 0, 0, 0, 2),
+    (0, 1, 0, 0, 1, 0, 1), (0, 0, 0, 0, 0, 0, -1), (0, 1, 0, 0, 0, 0, 1), (0, 1, 0, 0, 1, 0, -1), (0, 1, 0, 0, 0, 0, -1),
+    (0, 0, 0, 0, 0, 0, 1), (0, 0, 0, 0, 1, 0, -1), (1, 0, 0), (0, 0, 0, 0, 1, 1, 1), (0, 0, 0, 0, 1, 1, 2),
+    (0, 0, 0, 0, 0, 1, 2), (0, 1, 0, 0, 0, 1, 2), (0, 1, 0, 0, 1, 1, -1), (0, 1, 0, 0, 1, 1, 2), (0, 0, 0, 0, 1, 1, -1),
+    (1, 0, 1), (0, 1, 0, 0, 1, 1, 1), (0, 0, 0, 0, 0, 1, 1), (0, 1, 0, 0, 0, 1, 1), (0, 0, 0, 0, 0, 1, -1),
+    (0, 1, 0, 0, 0, 1, -1), (0, 0, 2, 0, 1, 1, 2), (0, 0, 2, 0, 1, 1, -1), (0, 0, 2, 0, 1, 1, 1), (0, 1, 2, 0, 1, 1, -1),
+    (0, 1, 2, 0, 1, 1, 2), (0, 0, 2, 0, 0, 1, 2), (0, 1, 2, 0, 0, 1, 2), (0, 1, 2, 0, 0, 1, -1), (0, 0, 2, 0, 0, 1, -1),
+    (0, 1, 2, 0, 0, 1, 1), (0, 0, 2, 0, 0, 1, 1), (1, 0, 2), (0, 1, 2, 0, 1, 1, 1), (0, 0, 3, 0, 0, 1, 2),
+    (0, 1, 3, 0, 1, 1, 2), (0, 0, 1, 0, 0, 1, 2), (0, 0, 3, 0, 1, 1, 2), (0, 1, 1, 0, 0, 1, 2), (0, 1, 3, 0, 0, 1, 2),
+    (0, 1, 1, 0, 1, 1, 2), (0, 0, 1, 0, 1, 1, 2), (0, 1, 1, 0, 1, 1, -1), (1, 3, 0), (1, 3, 1),
+    (1, 3, 2), (0, 0, 1, 0, 0, 1, -1), (0, 0, 3, 0, 1, 1, -1), (0, 0, 3, 0, 0, 1, -1), (0, 0, 3, 0, 0, 1, 1),
+    (0, 0, 1, 0, 1, 1, -1), (0, 1, 3, 0, 0, 1, -1), (0, 0, 1, 0, 0, 1, 1), (0, 0, 3, 0, 1, 1, 1), (0, 0, 1, 0, 1, 1, 1),
+    (1, 1, 2), (1, 1, 0), (0, 1, 1, 0, 0, 1, -1), (0, 1, 3, 0, 1, 1, 1), (0, 1, 3, 0, 1, 1, -1),
+    (0, 1, 3, 0, 0, 1, 1), (0, 1, 1, 0, 1, 1, 1), (0, 1, 1, 0, 0, 1, 1), (1, 1, 1), (1, 5, 0),
+    (1, 5, 2), (1, 5, 1), (1, 4, 0), (1, 4, 2), (1, 4, 1),
+    (1, 2, 0), (1, 2, 1), (2, 0), (3, 2, 1), (4, 1, 1, 2, 1),
+    (4, 0, 2, 1, 0), (4, 1, 1, 2, 0), (3, 2, 2), (4, 0, 2, 2, 0), (4, 1, 2, 2, 1),
+    (4, 0, 2, 2, 1), (4, 1, 2, 2, 0), (3, 2, 3), (4, 0, 2, 3, 1), (4, 1, 3, 2, 0),
+    (3, 1, 2), (4, 1, 3, 2, 1), (4, 0, 1, 2, 0), (4, 0, 1, 2, 1), (3, 3, 2),
+    (4, 0, 3, 2, 1), (4, 1, 2, 3, 1), (4, 1, 2, 1, 0), (4, 0, 3, 2, 0), (3, 0, 3),
+    (3, 0, 2), (3, 2, 0), (4, 1, 0, 2, 1), (4, 0, 0, 2, 1), (1, 2, 2),
+    (3, 3, 3), (3, 1, 1), (4, 0, 0, 2, 0), (4, 1, 3, 3, 1), (4, 1, 1, 1, 0),
+    (4, 1, 0, 2, 0), (3, 3, 1), (4, 0, 1, 1, 0), (4, 0, 2, 3, 0), (3, 1, 3),
+    (4, 1, 3, 1, 0), (4, 1, 1, 3, 0), (4, 1, 2, 1, 1), (4, 1, 1, 1, 1), (4, 0, 2, 1, 1),
+    (4, 0, 3, 3, 1), (4, 1, 3, 3, 0), (4, 1, 1, 3, 1), (4, 1, 2, 3, 0), (4, 0, 3, 1, 0),
+    (4, 1, 3, 1, 1), (5, 0), (4, 0, 1, 3, 0), (3, 1, 0), (4, 0, 1, 1, 1),
+    (3, 3, 0), (4, 0, 3, 3, 0), (4, 0, 3, 1, 1), (4, 0, 1, 3, 1), (3, 0, 0),
+    (4, 0, 0, 3, 1), (3, 0, 1), (5, 1), (4, 0, 0, 3, 0), (4, 0, 0, 1, 1),
+    (4, 0, 0, 1, 0), (4, 1, 0, 1, 1), (4, 1, 0, 3, 1), (4, 1, 0, 3, 0), (4, 1, 0, 1, 0),
+    (4, 1, 3, 0, 0), (4, 1, 1, 0, 0), (4, 1, 1, 0, 1), (4, 0, 2, 0, 0), (4, 1, 2, 0, 0),
+    (4, 0, 2, 0, 1), (4, 1, 2, 0, 1), (4, 0, 1, 0, 0), (4, 0, 3, 0, 0), (4, 0, 1, 0, 1),
+    (4, 1, 3, 0, 1), (4, 0, 3, 0, 1), (4, 1, 0, 0, 1), (4, 0, 0, 0, 1), (4, 1, 0, 0, 0),
+    (6, 0), (4, 0, 0, 0, 0), (6, 1),
 )
 NT = (((1,), (1,)), ((), ()))
 TN = (((0,), (0,)), ((), ()))
@@ -63,30 +67,28 @@
     return lax.dot_general(a, b, dims, preferred_element_type=jnp.float32)
 
 
-def frame(X, blk):
-    return blk if X == 0 else (blk[1], blk[0])
-
-
 def unframe(X, a, b):
     return (a, b) if X == 0 else (b, a)
 
 
-def terms(a, b, o):
-    if b == 3:
-        return [('rb', a, o)] if o == 0 else []
-    if b == 1:
-        return [('rb', a, o)] if o == 1 else []
+def side(o):
+    return -1 if o == 0 else 1
+
+
+def terms(X, a, b, o):
     if b == 2:
         return []
+    if b:
+        return [('rb', a, o)] if side(o) == (-1 if b == 3 else 1) else []
     out = [('fb', a, o, 1), ('fb', a, o, -1)]
-    if a == 0:
+    if a == 0 and o == 0:
         out += [('fa', o, 1), ('fa', o, -1), ('ra', o)]
     return out
 
 
-def target(a, b, o):
+def target(X, a, b, o):
     if b == 2:
-        return (0, -1 if o == 0 else 1), ('rb', a, o)
+        return (0, side(o)), ('rb', a, o)
     if b:
         return (0, -1 if b == 3 else 1), ('fb', a, o, 1 if b == 3 else -1)
     if a == 2:
@@ -99,13 +101,13 @@
     for _b in range(SIDE):
         for _o in range(CORES):
             if (_a, _b) != (0, 0):
-                RIDX[target(_a, _b, _o)[1]] = len(RIDX)
+                RIDX[target(0, _a, _b, _o)[1]] = len(RIDX)
 
 
 def kernel(cp, n_docs, scale, q_hbm, k_hbm, v_hbm, do_hbm, val_hbm, cu_hbm,
            o_out, lse_out, dq_out, dk_out, dv_out,
            kin, kf32, oth, kv, kaug, qbuf, qt, dob, dot_t, dot_b, sbuf, dpbuf, pbuf, dsbuf, part, rbuf,
-           ost, dqst, lsest, kvsend, kvrecv, tmp32, m_ref, l_ref, o_t, valv, cus,
+           ost, dqst, lsest, last, grad, tmp32, m_ref, l_ref, lse_v, lse2_v, delta_v, top, o_t, valv, cus,
            loc_sem, pair_send, pair_recv, ag_send, ag_recv, rs_send, rs_recv):
     tok = valv.shape[1]
     grp = ost.shape[0]
@@ -122,8 +124,8 @@
     def chip_at(dx, dy):
         return lax.rem(cy + dy + SIDE, SIDE) * SIDE + lax.rem(cx + dx + SIDE, SIDE)
 
-    def nbr(step):
-        return {'cp': chip_at(*step) * CORES + core}
+    def nbr(step, cross=False):
+        return {'cp': chip_at(*step) * CORES + (1 - core if cross else core)}
 
     mine = core * grp
     theirs = (1 - core) * grp
@@ -139,7 +141,8 @@
         c.start()
 
     barrier = pltpu.get_barrier_semaphore()
-    peers = [to_partner] + [nbr(s) for s in ((1, 0), (-1, 0), (2, 0), (0, 1), (0, -1), (0, 2))]
+    near = ((1, 0), (-1, 0), (2, 0), (0, 1), (0, -1), (0, 2))
+    peers = [to_partner] + [nbr(s, cross) for s in near for cross in (False, True)]
     for peer in peers:
         pl.semaphore_signal(barrier, inc=1, device_id=peer, device_id_type=MESH)
 
@@ -191,17 +194,20 @@
 
     def forward(X, a, b, o, phase, step):
         blk = unframe(X, a, b)
-        arrive(X, blk, o)
         step = unframe(X, step * (1 - phase), step * phase)
+        cross = blk == (0, 0) and o == 1
+        src = oth.at[X] if cross else kv.at[X, SLOT[blk], o]
+        if not cross:
+            arrive(X, blk, o)
         d = SLOT[(blk[0] - step[0]) % SIDE, (blk[1] - step[1]) % SIDE]
-        push(kv.at[X, SLOT[blk], o], kv.at[X, d, o], ag_send.at[ag_count[0]], ag_recv.at[X, d, o], nbr(step))
+        push(src, kv.at[X, d, o], ag_send.at[ag_count[0]], ag_recv.at[X, d, o], nbr(step, cross))
         ag_count[0] += 1
 
     for X in range(2):
         push(oth.at[X], kv.at[X, 0, 1], pair_send.at[X], ag_recv.at[X, 0, 1], to_partner)
     early = 0
-    while len(GATHER[early]) == 6 and GATHER[early][1:4] == (0, 0, 0):
-        forward(*GATHER[early])
+    while ORDER[early][0] == 0 and ORDER[early][2:4] == (0, 0):
+        forward(*ORDER[early][1:])
         early += 1
     x_q = push(q_hbm.at[pl.ds(theirs, grp)], qbuf.at[grp:2 * grp], pair_send.at[2], pair_recv.at[2], to_partner)
     x_do = push(do_hbm.at[pl.ds(theirs, grp)], dob.at[grp:2 * grp], pair_send.at[3], pair_recv.at[3], to_partner)
@@ -258,6 +264,7 @@
             prepare(blk)
         s = dot(kaug[lo:lo + n].reshape(n * keys, 2 * hd), qt[...])
         sbuf[lo:lo + n] = s.reshape(n, keys, rows)
+        top[lo:lo + 1] = jnp.max(s, axis=0, keepdims=True)
 
     def grads_p(group):
         lo, n = SLOT[group[0]], len(group)
@@ -266,7 +273,7 @@
 
     def softmax(group, first):
         lo, n = SLOT[group[0]], len(group)
-        mx = jnp.max(sbuf[lo:lo + n].reshape(n * keys, rows), axis=0, keepdims=True)
+        mx = top[lo:lo + 1]
         if first:
             m_new = mx
         else:
@@ -289,55 +296,21 @@
             l_ref[...] = l_ref[...] * alpha + total
             o_t[...] = o_t[...] * alpha + pv
 
-    started = [False, False, False]
-    for item in GATHER[early:]:
-        if len(item) == 6:
-            with scope('fwd%d_%d%d_%d' % item[:4]):
-                forward(*item)
-            continue
-        gi, stage = item
-        group = GROUPS[gi]
-        with scope('wait%d_%d' % item):
-            for blk in group:
-                for o in range(CORES):
-                    arrive(min(stage, 1), blk, o)
-            if not started[0]:
-                c_q.wait()
-                x_q.wait_recv()
-                qt[0:hd, :] = jnp.transpose(qbuf[...].reshape(rows, hd).astype(jnp.float32)).astype(jnp.bfloat16)
-                started[0] = True
-            if stage == 2 and not started[1]:
-                c_do.wait()
-                x_do.wait_recv()
-                do_t = jnp.transpose(dob[...].reshape(rows, hd).astype(jnp.float32))
-                dot_t[...] = do_t
-                dot_b[...] = do_t.astype(jnp.bfloat16)
-                started[1] = True
-        with scope('group%d_%d' % item):
-            if stage == 0:
-                scores(group)
-            elif stage == 1:
-                softmax(group, not started[2])
-                started[2] = True
-            else:
-                grads_p(group)
-
-    scope_fin = scope('finish')
-    scope_fin.__enter__()
-    m_fin, l_fin = m_ref[...], l_ref[...]
-    has_key = m_fin > NEG * 0.5
-    safe = jnp.where(has_key, l_fin, 1.0)
-    o_b = jnp.where(has_key, o_t[...] / safe, 0.0).astype(jnp.bfloat16).astype(jnp.float32)
-    o_t[...] = o_b
-    delta = jnp.sum(o_b * dot_t[...], axis=0, keepdims=True)
-    lse = jnp.where(has_key, m_fin * scale + jnp.log(safe), 0.0)
-    lse2 = jnp.where(has_key, m_fin * c2 + jnp.log2(safe), 0.0)
-
-    scope_fin.__exit__(None, None, None)
-
-    def rsend(X, blk, o, key, step):
+    def row_terms():
+        m_fin, l_fin = m_ref[...], l_ref[...]
+        has_key = m_fin > NEG * 0.5
+        safe = jnp.where(has_key, l_fin, 1.0)
+        o_b = jnp.where(has_key, o_t[...] / safe, 0.0).astype(jnp.bfloat16).astype(jnp.float32)
+        o_t[...] = o_b
+        delta_v[...] = jnp.sum(o_b * dot_t[...], axis=0, keepdims=True)
+        lse_v[...] = jnp.where(has_key, m_fin * scale + jnp.log(safe), 0.0)
+        lse2_v[...] = jnp.where(has_key, m_fin * c2 + jnp.log2(safe), 0.0)
+
+    def rsend(X, a, b, o):
+        step, key = target(X, a, b, o)
         i = RIDX[key]
-        push(part.at[X, SLOT[blk], o], rbuf.at[X, i], rs_send.at[X, i], rs_recv.at[X, i], nbr(unframe(X, *step)))
+        dev = nbr(unframe(X, *step), b == 0 and o == 1)
+        push(part.at[X, SLOT[unframe(X, a, b)], o], rbuf.at[X, i], rs_send.at[X, i], rs_recv.at[X, i], dev)
 
     def rwait(X, key):
         i = RIDX[key]
@@ -346,18 +319,18 @@
 
     def total(X, a, b, o):
         s = SLOT[unframe(X, a, b)]
-        keys_in = terms(a, b, o)
-        if keys_in:
+        names = terms(X, a, b, o)
+        if names:
             acc = part[X, s, o]
-            for key in keys_in:
-                acc = acc + rwait(X, key)
+            for name in names:
+                acc = acc + rwait(X, name)
             part[X, s, o] = acc
 
     def backward(blk):
         s = SLOT[blk]
-        p = jnp.exp2(sbuf[s] * c2 - lse2)
+        p = jnp.exp2(sbuf[s] * c2 - lse2_v[...])
         pbuf[s] = p.astype(jnp.bfloat16)
-        dsbuf[s] = (p * (dpbuf[s] - delta)).astype(jnp.bfloat16)
+        dsbuf[s] = (p * (dpbuf[s] - delta_v[...])).astype(jnp.bfloat16)
         part[1, s] = dot(pbuf[s], dob[...].reshape(rows, hd)).reshape(CORES, tok, hd)
         part[0, s] = dot(dsbuf[s], qbuf[...].reshape(rows, hd)).reshape(CORES, tok, hd)
 
@@ -368,8 +341,8 @@
         o_out[pl.ds(mine, grp)] = o_rows[0:grp]
         ost[...] = o_rows[grp:2 * grp]
         for h in range(grp):
-            lse_out[core, h:h + 1, :] = lse[:, h * tok:(h + 1) * tok]
-            lsest[h:h + 1, :] = lse[:, (grp + h) * tok:(grp + h + 1) * tok]
+            lse_out[core, h:h + 1, :] = lse_v[:, h * tok:(h + 1) * tok]
+            lsest[h:h + 1, :] = lse_v[:, (grp + h) * tok:(grp + h + 1) * tok]
         x_out.append(push(ost, o_out.at[pl.ds(mine, grp)], pair_send.at[4], pair_recv.at[4], to_partner))
         x_out.append(push(lsest, lse_out.at[core], pair_send.at[5], pair_recv.at[5], to_partner))
 
@@ -380,44 +353,90 @@
         dqst[...] = dq_rows[grp:2 * grp]
         x_out.append(push(dqst, dq_out.at[pl.ds(mine, grp)], pair_send.at[6], pair_recv.at[6], to_partner))
 
-    x_kv, owns = {}, {}
+    x_sum = {}
 
     def finish(X, o):
         total(X, 0, 0, o)
-        res = part[X, 0, o] * scale if X == 0 else part[X, 0, o]
         if o == 1:
-            kvsend[X] = res.astype(jnp.bfloat16)
-            x_kv[X] = push(kvsend.at[X], kvrecv.at[X], pair_send.at[7 + X], pair_recv.at[7 + X], to_partner)
+            x_sum[X] = push(part.at[X, 0, 1], last.at[X], pair_send.at[7 + X], pair_recv.at[7 + X], to_partner)
         else:
-            owns[X] = res.astype(jnp.bfloat16).astype(jnp.float32)
-
-    for item in SCATTER:
-        if len(item) == 3:
-            with scope('late%d_%d' % item[:2]):
-                grads_p(GROUPS[item[0]])
-        elif len(item) == 2:
-            with scope('bwd%d%d' % item):
-                backward(item)
-        elif len(item) == 1:
-            with scope('store%d' % item):
+            grad[X, 0] = part[X, 0, 0] * scale if X == 0 else part[X, 0, 0]
+
+    def finish_other(X):
+        x_sum[X].wait_recv()
+        acc = last[X]
+        for name in (('fa', 1, 1), ('fa', 1, -1), ('ra', 1)):
+            acc = acc + rwait(X, name)
+        grad[X, 1] = acc * scale if X == 0 else acc
+
+    def need_q():
+        if 'q' not in ready:
+            ready.add('q')
+            c_q.wait()
+            x_q.wait_recv()
+            qt[0:hd, :] = jnp.transpose(qbuf[...].reshape(rows, hd).astype(jnp.float32)).astype(jnp.bfloat16)
+
+    def need_do():
+        if 'do' not in ready:
+            ready.add('do')
+            c_do.wait()
+            x_do.wait_recv()
+            do_t = jnp.transpose(dob[...].reshape(rows, hd).astype(jnp.float32))
+            dot_t[...] = do_t
+            dot_b[...] = do_t.astype(jnp.bfloat16)
+
+    def group_part(gi, stage):
+        group = GROUPS[gi]
+        first = stage not in ready
+        ready.add(stage)
+        with scope('wait%d_%d' % (gi, stage)):
+            for blk in group:
+                for o in range(CORES):
+                    arrive(min(stage, 1), blk, o)
+            if stage == 0:
+                need_q()
+            elif stage == 2:
+                need_do()
+        with scope('group%d_%d' % (gi, stage)):
+            if stage == 0:
+                scores(group)
+            elif stage == 1:
+                softmax(group, first)
+            else:
+                grads_p(group)
+
+    def pass_on(X, a, b, o):
+        if (a, b) == (0, 0):
+            finish(X, o)
+        else:
+            total(X, a, b, o)
+            rsend(X, a, b, o)
+
+    ready = set()
+    for code, *item in ORDER[early:]:
+        with scope('%d_' % code + '_'.join(map(str, item))):
+            if code == 0:
+                forward(*item)
+            elif code == 1:
+                group_part(*item)
+            elif code == 2:
+                need_do()
+                row_terms()
+            elif code == 3:
+                backward(tuple(item))
+            elif code == 4:
+                pass_on(*item)
+            elif code == 5:
                 (store_o, store_dq)[item[0]]()
-        elif item[1:3] == (0, 0):
-            with scope('final%d_%d' % (item[0], item[3])):
-                finish(item[0], item[3])
-        else:
-            X, a, b, o = item
-            with scope('sum%d_%d%d_%d' % item):
-                total(X, a, b, o)
-                step, key = target(a, b, o)
-                rsend(X, unframe(X, a, b), o, key, step)
+            else:
+                finish_other(*item)
 
     scope_out = scope('tail')
     scope_out.__enter__()
     for X, out in ((0, dk_out), (1, dv_out)):
-        x_kv[X].wait_recv()
-        got = kvrecv[X].astype(jnp.float32)
-        tmp32[X, pl.ds(0, tok, stride=2), :] = jnp.where(core == 0, owns[X], got)
-        tmp32[X, pl.ds(1, tok, stride=2), :] = jnp.where(core == 0, got, owns[X])
+        own, other = grad[X, 0], grad[X, 1]
+        tmp32[X, pl.ds(0, tok, stride=2), :] = jnp.where(core == 0, own, other)
+        tmp32[X, pl.ds(1, tok, stride=2), :] = jnp.where(core == 0, other, own)
         out[...] = tmp32[X].astype(jnp.bfloat16)
     for c in sends:
         c.wait_send()
@@ -488,11 +507,15 @@
                 pltpu.VMEM((grp, tok, hd), bf),
                 pltpu.VMEM((grp, tok, hd), bf),
                 pltpu.VMEM((grp, tok), f32),
-                pltpu.VMEM((2, tok, hd), bf),
-                pltpu.VMEM((2, tok, hd), bf),
+                pltpu.VMEM((2, tok, hd), f32),
+                pltpu.VMEM((2, 2, tok, hd), f32),
                 pltpu.VMEM((2, tok * kvh, hd), f32),
                 pltpu.VMEM((1, rows), f32),
                 pltpu.VMEM((1, rows), f32),
+                pltpu.VMEM((1, rows), f32),
+                pltpu.VMEM((1, rows), f32),
+                pltpu.VMEM((1, rows), f32),
+                pltpu.VMEM((NBLK, rows), f32),
                 pltpu.VMEM((hd, rows), f32),
                 pltpu.VMEM((1, tok), jnp.int32),
                 pltpu.SMEM((1, n_docs + 1), jnp.int32),

time: 39 us -> 37.2 us (0.954)
  Pallas kernels: 38.3 us -> 36.4 us
    pallas_call x1, Pallas kernels: 37.5 us -> 35.6 us  [local(): pl.pallas_call(functools.partial(kernel, cp, n_docs, hd ** (-0.5)), name=...]
where the time goes in v4:
time: 37.2 us; the launch traced here: 37.1 us
  Pallas kernels  36.4 us (98%)
  between operations  0.64 us (2%)
    pallas_call x1, Pallas kernels, local(): pl.pallas_call(functools.partial(kernel, cp, n_docs, hd ** (-0.5)), name=...  35.6 us
    pallas_call x1, Pallas kernels, local(): pl.pallas_call(store_kernel, name='store_outputs', out_shape=[jax.ShapeDt...  0.8 us

profile of v4, /device:TPU:97, one launch (start us, length us, event | category | flops | bytes accessed | tf_op | source)
XLA Modules:
  0.0 37.1 jit_solution(13826426105219359703)
XLA Ops:
  0.6 35.6 %ring_attention.1 = (bf16[12,64,128]{2,1,0:T(8,128)(2,1)S(1)}, f32[2,6,64]{2,1,0:T(8,128)S(1)}, bf16[12,64,128]{2,1,0:T(8,128)(2,1)S(1)}, bf16[128,128]{1,0:T(8,128)(2,1)S(1)}, bf16[128,128]{1,0:T(8,128)(2,1)S(1)}) custom-call(bf16[12,64,128]{2,1,0:T(8,128)(2,1)} %bitcast.11, bf16[128,128]{1,0:T(8,128)(2,1)} %bitcast.13, bf16[128,128]{1,0:T(8,128)(2,1)} %bitcast.14, ...), custom_call_target="tpu_custom_call" | custom-call | tf_op jit(solution)/shard_map/ring_attention/pallas_call | solution.py:478
  36.3 0.8 %store_outputs.1 = (bf16[12,64,128]{2,1,0:T(8,128)(2,1)}, f32[12,64]{1,0:T(8,128)}, bf16[12,64,128]{2,1,0:T(8,128)(2,1)}, bf16[128,128]{1,0:T(8,128)(2,1)}, bf16[128,128]{1,0:T(8,128)(2,1)}) custom-call(bf16[12,64,128]{2,1,0:T(8,128)(2,1)S(1)} %get-tuple-element.15.o_in, f32[2,6,64]{2,1,0:T(8,128)S(1)} %get-tuple-element.16.lse_in, ...), custom_call_target="tpu_custom_call" | custom-call | tf_op jit(solution)/shard_map/store_outputs/pallas_call | solution.py:533

commit v5 on v4

--- a/solution.py
+++ b/solution.py
@@ -24,41 +24,37 @@
 BLOCKS = tuple(blk for group in GROUPS for blk in group)
 SLOT = {blk: i for i, blk in enumerate(BLOCKS)}
 NBLK = len(BLOCKS)
-ORDER = (
-    (0, 0, 0, 0, 1, 0, 2), (0, 1, 0, 0, 1, 0, 2), (0, 1, 0, 0, 0, 0, 2), (0, 0, 0, 0, 1, 0, 1), (0, 0, 0, 0, 0, 0, 2),
-    (0, 1, 0, 0, 1, 0, 1), (0, 0, 0, 0, 0, 0, -1), (0, 1, 0, 0, 0, 0, 1), (0, 1, 0, 0, 1, 0, -1), (0, 1, 0, 0, 0, 0, -1),
-    (0, 0, 0, 0, 0, 0, 1), (0, 0, 0, 0, 1, 0, -1), (1, 0, 0), (0, 0, 0, 0, 1, 1, 1), (0, 0, 0, 0, 1, 1, 2),
-    (0, 0, 0, 0, 0, 1, 2), (0, 1, 0, 0, 0, 1, 2), (0, 1, 0, 0, 1, 1, -1), (0, 1, 0, 0, 1, 1, 2), (0, 0, 0, 0, 1, 1, -1),
-    (1, 0, 1), (0, 1, 0, 0, 1, 1, 1), (0, 0, 0, 0, 0, 1, 1), (0, 1, 0, 0, 0, 1, 1), (0, 0, 0, 0, 0, 1, -1),
-    (0, 1, 0, 0, 0, 1, -1), (0, 0, 2, 0, 1, 1, 2), (0, 0, 2, 0, 1, 1, -1), (0, 0, 2, 0, 1, 1, 1), (0, 1, 2, 0, 1, 1, -1),
-    (0, 1, 2, 0, 1, 1, 2), (0, 0, 2, 0, 0, 1, 2), (0, 1, 2, 0, 0, 1, 2), (0, 1, 2, 0, 0, 1, -1), (0, 0, 2, 0, 0, 1, -1),
-    (0, 1, 2, 0, 0, 1, 1), (0, 0, 2, 0, 0, 1, 1), (1, 0, 2), (0, 1, 2, 0, 1, 1, 1), (0, 0, 3, 0, 0, 1, 2),
-    (0, 1, 3, 0, 1, 1, 2), (0, 0, 1, 0, 0, 1, 2), (0, 0, 3, 0, 1, 1, 2), (0, 1, 1, 0, 0, 1, 2), (0, 1, 3, 0, 0, 1, 2),
-    (0, 1, 1, 0, 1, 1, 2), (0, 0, 1, 0, 1, 1, 2), (0, 1, 1, 0, 1, 1, -1), (1, 3, 0), (1, 3, 1),
-    (1, 3, 2), (0, 0, 1, 0, 0, 1, -1), (0, 0, 3, 0, 1, 1, -1), (0, 0, 3, 0, 0, 1, -1), (0, 0, 3, 0, 0, 1, 1),
-    (0, 0, 1, 0, 1, 1, -1), (0, 1, 3, 0, 0, 1, -1), (0, 0, 1, 0, 0, 1, 1), (0, 0, 3, 0, 1, 1, 1), (0, 0, 1, 0, 1, 1, 1),
-    (1, 1, 2), (1, 1, 0), (0, 1, 1, 0, 0, 1, -1), (0, 1, 3, 0, 1, 1, 1), (0, 1, 3, 0, 1, 1, -1),
-    (0, 1, 3, 0, 0, 1, 1), (0, 1, 1, 0, 1, 1, 1), (0, 1, 1, 0, 0, 1, 1), (1, 1, 1), (1, 5, 0),
-    (1, 5, 2), (1, 5, 1), (1, 4, 0), (1, 4, 2), (1, 4, 1),
-    (1, 2, 0), (1, 2, 1), (2, 0), (3, 2, 1), (4, 1, 1, 2, 1),
-    (4, 0, 2, 1, 0), (4, 1, 1, 2, 0), (3, 2, 2), (4, 0, 2, 2, 0), (4, 1, 2, 2, 1),
-    (4, 0, 2, 2, 1), (4, 1, 2, 2, 0), (3, 2, 3), (4, 0, 2, 3, 1), (4, 1, 3, 2, 0),
-    (3, 1, 2), (4, 1, 3, 2, 1), (4, 0, 1, 2, 0), (4, 0, 1, 2, 1), (3, 3, 2),
-    (4, 0, 3, 2, 1), (4, 1, 2, 3, 1), (4, 1, 2, 1, 0), (4, 0, 3, 2, 0), (3, 0, 3),
-    (3, 0, 2), (3, 2, 0), (4, 1, 0, 2, 1), (4, 0, 0, 2, 1), (1, 2, 2),
-    (3, 3, 3), (3, 1, 1), (4, 0, 0, 2, 0), (4, 1, 3, 3, 1), (4, 1, 1, 1, 0),
-    (4, 1, 0, 2, 0), (3, 3, 1), (4, 0, 1, 1, 0), (4, 0, 2, 3, 0), (3, 1, 3),
-    (4, 1, 3, 1, 0), (4, 1, 1, 3, 0), (4, 1, 2, 1, 1), (4, 1, 1, 1, 1), (4, 0, 2, 1, 1),
-    (4, 0, 3, 3, 1), (4, 1, 3, 3, 0), (4, 1, 1, 3, 1), (4, 1, 2, 3, 0), (4, 0, 3, 1, 0),
-    (4, 1, 3, 1, 1), (5, 0), (4, 0, 1, 3, 0), (3, 1, 0), (4, 0, 1, 1, 1),
-    (3, 3, 0), (4, 0, 3, 3, 0), (4, 0, 3, 1, 1), (4, 0, 1, 3, 1), (3, 0, 0),
-    (4, 0, 0, 3, 1), (3, 0, 1), (5, 1), (4, 0, 0, 3, 0), (4, 0, 0, 1, 1),
-    (4, 0, 0, 1, 0), (4, 1, 0, 1, 1), (4, 1, 0, 3, 1), (4, 1, 0, 3, 0), (4, 1, 0, 1, 0),
-    (4, 1, 3, 0, 0), (4, 1, 1, 0, 0), (4, 1, 1, 0, 1), (4, 0, 2, 0, 0), (4, 1, 2, 0, 0),
-    (4, 0, 2, 0, 1), (4, 1, 2, 0, 1), (4, 0, 1, 0, 0), (4, 0, 3, 0, 0), (4, 0, 1, 0, 1),
-    (4, 1, 3, 0, 1), (4, 0, 3, 0, 1), (4, 1, 0, 0, 1), (4, 0, 0, 0, 1), (4, 1, 0, 0, 0),
-    (6, 0), (4, 0, 0, 0, 0), (6, 1),
-)
+
+
+def all_tasks():
+    far = (2, 1, 3, 0)
+    tasks = []
+    for X in range(2):
+        for o in range(CORES):
+            tasks += [(0, X, 0, 0, o, 0, step) for step in (1, -1, 2)]
+            for a in range(SIDE):
+                for step in (1, -1, 2):
+                    if step == 2 and a in RELAYED:
+                        tasks.append((0, X, a, 3 if o == 0 else 1, o, 1, 1 if o == 0 else -1))
+                    else:
+                        tasks.append((0, X, a, 0, o, 1, step))
+    tasks += [(1, g, stage) for g in range(len(GROUPS)) for stage in range(3)] + [(2, 0)]
+    tasks += [(3,) + blk for blk in BLOCKS] + [(5, 0), (5, 1)]
+    for X in range(2):
+        for o in range(CORES):
+            tasks += [(4, X, a, b, o) for b in far for a in far]
+        tasks.append((6, X))
+    return tasks
+
+
+RELAYED = ()
+ORDER = tuple(all_tasks()[i] for i in dict.fromkeys(b for n in (
+    0x112f200f022d011e2e1f, 0x00103c12140523313213, 0x3d30032104221a191837, 0x380b29280a27093e360e,
+    0x3b081d262c3517344546, 0x47071c0d0c162b061b15, 0x413f25393a2a3324404b, 0x4d4c484a4942434e5a93,
+    0x65835e619271825b7984, 0x5c9462725d739a866353, 0x59589574445754649c87, 0x8556666955888b969775,
+    0x7b8c9b8a67985f6a5076, 0x516b777a4f7c52606c78, 0x68999d8d89908f9f6d8e, 0x7d9e6e6f7ea07fa18091,
+    0x8170a2a2a2a2a2a2a2a2,
+) for b in n.to_bytes(10, 'big')))
 NT = (((1,), (1,)), ((), ()))
 TN = (((0,), (0,)), ((), ()))
 
@@ -102,15 +98,46 @@
         for _o in range(CORES):
             if (_a, _b) != (0, 0):
                 RIDX[target(0, _a, _b, _o)[1]] = len(RIDX)
+RIDX['lo', 1] = len(RIDX)
+
+
+def consumer(key):
+    if key[0] == 'rb':
+        return key
+    if key[0] == 'fb':
+        return ('sum',) + key[1:3]
+    return ('sum', 0, 0) if key[1] == 0 else ('other',)
+
+
+RSEM, RNUM = {}, {}
+for _key in RIDX:
+    RSEM.setdefault(consumer(_key), len(RSEM))
+    RNUM[consumer(_key)] = RNUM.get(consumer(_key), 0) + 1
+
+
+def passes_on(X, blk):
+    return unframe(X, *blk)[1] == 0 or (unframe(X, *blk)[1] != 2 and unframe(X, *blk)[0] in RELAYED)
+
+
+ASEM, ANUM = {}, {}
+for _X in range(2):
+    for _g, _group in enumerate(GROUPS):
+        for _blk in _group:
+            for _o in range(CORES):
+                if _blk != (0, 0) or _o == 1:
+                    _name = (_X, _blk, _o) if passes_on(_X, _blk) else (_X, _g)
+                    ASEM[_X, _blk, _o] = _name
+                    ANUM[_name] = ANUM.get(_name, 0) + 1
+AIDX = {name: i for i, name in enumerate(ANUM)}
 
 
 def kernel(cp, n_docs, scale, q_hbm, k_hbm, v_hbm, do_hbm, val_hbm, cu_hbm,
            o_out, lse_out, dq_out, dk_out, dv_out,
            kin, kf32, oth, kv, kaug, qbuf, qt, dob, dot_t, dot_b, sbuf, dpbuf, pbuf, dsbuf, part, rbuf,
-           ost, dqst, lsest, last, grad, tmp32, m_ref, l_ref, lse_v, lse2_v, delta_v, top, o_t, valv, cus,
+           ost, dqst, lsest, grad, tmp32, outb, lse_all, m_ref, l_ref, lse_v, lse2_v, delta_v, top, o_t, valv, cus,
            loc_sem, pair_send, pair_recv, ag_send, ag_recv, rs_send, rs_recv):
     tok = valv.shape[1]
-    grp = ost.shape[0]
+    grp = ost.shape[0] // CORES
     rows = CORES * grp * tok
     hd = kin.shape[-1]
     keys = CORES * tok
@@ -131,22 +158,21 @@
     theirs = (1 - core) * grp
     to_partner = {'cp': partner}
 
-    c_k = pltpu.make_async_copy(k_hbm, kin.at[0], loc_sem.at[0])
-    c_v = pltpu.make_async_copy(v_hbm, kin.at[1], loc_sem.at[1])
-    c_val = pltpu.make_async_copy(val_hbm, valv, loc_sem.at[2])
-    c_cu = pltpu.make_async_copy(cu_hbm, cus, loc_sem.at[3])
-    c_q = pltpu.make_async_copy(q_hbm.at[pl.ds(mine, grp)], qbuf.at[0:grp], loc_sem.at[4])
-    c_do = pltpu.make_async_copy(do_hbm.at[pl.ds(mine, grp)], dob.at[0:grp], loc_sem.at[5])
-    for c in (c_k, c_v, c_val, c_cu, c_q, c_do):
-        c.start()
-
     barrier = pltpu.get_barrier_semaphore()
     near = ((1, 0), (-1, 0), (2, 0), (0, 1), (0, -1), (0, 2))
     peers = [to_partner] + [nbr(s, cross) for s in near for cross in (False, True)]
     for peer in peers:
         pl.semaphore_signal(barrier, inc=1, device_id=peer, device_id_type=MESH)
 
-    sends = []
+    c_k = pltpu.make_async_copy(k_hbm, kin.at[0], loc_sem.at[0])
+    c_v = pltpu.make_async_copy(v_hbm, kin.at[1], loc_sem.at[0])
+    c_kv = pltpu.make_async_copy(kin, kin, loc_sem.at[0])
+    c_val = pltpu.make_async_copy(val_hbm, valv, loc_sem.at[1])
+    c_cu = pltpu.make_async_copy(cu_hbm, cus, loc_sem.at[2])
+    c_q = pltpu.make_async_copy(q_hbm.at[pl.ds(mine, grp)], qbuf.at[0:grp], loc_sem.at[3])
+    c_do = pltpu.make_async_copy(do_hbm.at[pl.ds(mine, grp)], dob.at[0:grp], loc_sem.at[4])
+    for c in (c_k, c_v, c_val, c_cu, c_q, c_do):
+        c.start()
 
     def remote(src, dst, ssem, rsem, dev):
         copy = pltpu.make_async_remote_copy(src_ref=src, dst_ref=dst, send_sem=ssem, recv_sem=rsem,
@@ -156,11 +182,10 @@
     def push(src, dst, ssem, rsem, dev):
         copy = remote(src, dst, ssem, rsem, dev)
         copy.start()
-        sends.append(copy)
         return copy
 
     with scope('load_kv'):
-        for c in (c_k, c_v, c_val):
+        for c in (c_kv, c_val):
             c.wait()
     sub = lax.broadcasted_iota(jnp.int32, (tok, tok), 0)
     lane = lax.broadcasted_iota(jnp.int32, (tok, tok), 1)
@@ -184,13 +209,17 @@
         pl.semaphore_wait(barrier, len(peers))
 
     here = {(X, (0, 0), 0) for X in range(2)}
-    ag_count = [0]
+
+    def arrival(X, blk, o):
+        return ag_recv.at[AIDX[ASEM[X, blk, o]]]
 
     def arrive(X, blk, o):
         if (X, blk, o) not in here:
-            s = SLOT[blk]
-            remote(kv.at[X, s, o], kv.at[X, s, o], ag_send.at[0], ag_recv.at[X, s, o], to_partner).wait_recv()
-            here.add((X, blk, o))
+            name = ASEM[X, blk, o]
+            n = ANUM[name]
+            ref = kv.at[0, 0, 0] if n == 1 else kv.at[0, 0:n // 2]
+            remote(ref, ref, ag_send, arrival(X, blk, o), to_partner).wait_recv()
+            here.update(k for k, v in ASEM.items() if v == name)
 
     def forward(X, a, b, o, phase, step):
         blk = unframe(X, a, b)
@@ -200,17 +229,17 @@
         if not cross:
             arrive(X, blk, o)
         d = SLOT[(blk[0] - step[0]) % SIDE, (blk[1] - step[1]) % SIDE]
-        push(src, kv.at[X, d, o], ag_send.at[ag_count[0]], ag_recv.at[X, d, o], nbr(step, cross))
-        ag_count[0] += 1
+        d_blk = BLOCKS[d]
+        push(src, kv.at[X, d, o], ag_send, arrival(X, d_blk, o), nbr(step, cross))
 
     for X in range(2):
-        push(oth.at[X], kv.at[X, 0, 1], pair_send.at[X], ag_recv.at[X, 0, 1], to_partner)
+        push(oth.at[X], kv.at[X, 0, 1], ag_send, arrival(X, (0, 0), 1), to_partner)
     early = 0
     while ORDER[early][0] == 0 and ORDER[early][2:4] == (0, 0):
         forward(*ORDER[early][1:])
         early += 1
-    x_q = push(q_hbm.at[pl.ds(theirs, grp)], qbuf.at[grp:2 * grp], pair_send.at[2], pair_recv.at[2], to_partner)
-    x_do = push(do_hbm.at[pl.ds(theirs, grp)], dob.at[grp:2 * grp], pair_send.at[3], pair_recv.at[3], to_partner)
+    x_q = push(q_hbm.at[pl.ds(theirs, grp)], qbuf.at[grp:2 * grp], pair_send.at[0], pair_recv.at[0], to_partner)
+    x_do = push(do_hbm.at[pl.ds(theirs, grp)], dob.at[grp:2 * grp], pair_send.at[0], pair_recv.at[1], to_partner)
 
     t_row = lax.broadcasted_iota(jnp.int32, (tok, hd), 0)
     t_sub = lax.broadcasted_iota(jnp.int32, (keys, rows), 0)
@@ -310,20 +339,22 @@
         step, key = target(X, a, b, o)
         i = RIDX[key]
         dev = nbr(unframe(X, *step), b == 0 and o == 1)
-        push(part.at[X, SLOT[unframe(X, a, b)], o], rbuf.at[X, i], rs_send.at[X, i], rs_recv.at[X, i], dev)
-
-    def rwait(X, key):
-        i = RIDX[key]
-        remote(rbuf.at[X, i], rbuf.at[X, i], rs_send.at[X, i], rs_recv.at[X, i], to_partner).wait_recv()
-        return rbuf[X, i]
+        push(part.at[X, SLOT[unframe(X, a, b)], o], rbuf.at[X, i], rs_send, rs_recv.at[X, RSEM[consumer(key)]], dev)
+
+    def rwait(X, names):
+        name = consumer(names[0])
+        assert len(names) == RNUM[name]
+        ref = rbuf.at[X, 0:len(names)]
+        remote(ref, ref, rs_send, rs_recv.at[X, RSEM[name]], to_partner).wait_recv()
+        return [rbuf[X, RIDX[key]] for key in names]
 
     def total(X, a, b, o):
         s = SLOT[unframe(X, a, b)]
         names = terms(X, a, b, o)
         if names:
             acc = part[X, s, o]
-            for name in names:
-                acc = acc + rwait(X, name)
+            for term in rwait(X, names):
+                acc = acc + term
             part[X, s, o] = acc
 
     def backward(blk):
@@ -334,39 +365,41 @@
         part[1, s] = dot(pbuf[s], dob[...].reshape(rows, hd)).reshape(CORES, tok, hd)
         part[0, s] = dot(dsbuf[s], qbuf[...].reshape(rows, hd)).reshape(CORES, tok, hd)
 
-    x_out = []
+    x_out, x_lse = [], []
+
+    local = []
+
+    def store(src, dst, i):
+        c = pltpu.make_async_copy(src, dst, loc_sem.at[i])
+        c.start()
+        local.append(c)
 
     def store_o():
-        o_rows = jnp.transpose(o_t[...]).astype(jnp.bfloat16).reshape(2 * grp, tok, hd)
-        o_out[pl.ds(mine, grp)] = o_rows[0:grp]
-        ost[...] = o_rows[grp:2 * grp]
-        for h in range(grp):
-            lse_out[core, h:h + 1, :] = lse_v[:, h * tok:(h + 1) * tok]
-            lsest[h:h + 1, :] = lse_v[:, (grp + h) * tok:(grp + h + 1) * tok]
-        x_out.append(push(ost, o_out.at[pl.ds(mine, grp)], pair_send.at[4], pair_recv.at[4], to_partner))
-        x_out.append(push(lsest, lse_out.at[core], pair_send.at[5], pair_recv.at[5], to_partner))
+        ost[...] = jnp.transpose(o_t[...]).astype(jnp.bfloat16).reshape(2 * grp, tok, hd)
+        for i in range(CORES):
+            for h in range(grp):
+                j = (i * grp + h) * tok
+                lsest[i, h:h + 1, :] = lse_v[:, j:j + tok]
+        store(ost.at[0:grp], o_out.at[pl.ds(mine, grp)], 0)
+        x_out.append(push(ost.at[grp:2 * grp], o_out.at[pl.ds(mine, grp)], pair_send.at[0], pair_recv.at[2], to_partner))
+        x_lse.append(push(lsest.at[1], lsest.at[2], pair_send.at[1], pair_recv.at[3], to_partner))
 
     def store_dq():
         dq_t = dot(kaug[:, :, 0:hd].reshape(NBLK * keys, hd), dsbuf[...].reshape(NBLK * keys, rows), TN)
-        dq_rows = (jnp.transpose(dq_t) * scale).astype(jnp.bfloat16).reshape(2 * grp, tok, hd)
-        dq_out[pl.ds(mine, grp)] = dq_rows[0:grp]
-        dqst[...] = dq_rows[grp:2 * grp]
-        x_out.append(push(dqst, dq_out.at[pl.ds(mine, grp)], pair_send.at[6], pair_recv.at[6], to_partner))
-
-    x_sum = {}
+        dqst[...] = (jnp.transpose(dq_t) * scale).astype(jnp.bfloat16).reshape(2 * grp, tok, hd)
+        store(dqst.at[0:grp], dq_out.at[pl.ds(mine, grp)], 1)
+        x_out.append(push(dqst.at[grp:2 * grp], dq_out.at[pl.ds(mine, grp)], pair_send.at[0], pair_recv.at[2], to_partner))
 
     def finish(X, o):
         total(X, 0, 0, o)
         if o == 1:
-            x_sum[X] = push(part.at[X, 0, 1], last.at[X], pair_send.at[7 + X], pair_recv.at[7 + X], to_partner)
+            key = ('lo', 1)
+            push(part.at[X, 0, 1], rbuf.at[X, RIDX[key]], rs_send, rs_recv.at[X, RSEM[consumer(key)]], to_partner)
         else:
             grad[X, 0] = part[X, 0, 0] * scale if X == 0 else part[X, 0, 0]
 
     def finish_other(X):
-        x_sum[X].wait_recv()
-        acc = last[X]
-        for name in (('fa', 1, 1), ('fa', 1, -1), ('ra', 1)):
-            acc = acc + rwait(X, name)
+        acc = sum(rwait(X, (('lo', 1), ('fa', 1, 1), ('fa', 1, -1), ('ra', 1))))
         grad[X, 1] = acc * scale if X == 0 else acc
 
     def need_q():
@@ -433,27 +466,30 @@
 
     scope_out = scope('tail')
     scope_out.__enter__()
+    x_lse[0].wait_recv()
+    lse_all[0:grp] = jnp.where(core == 0, lsest[0], lsest[2])
+    lse_all[grp:2 * grp] = jnp.where(core == 0, lsest[2], lsest[0])
+    store(lse_all, lse_out, 4)
     for X, out in ((0, dk_out), (1, dv_out)):
         own, other = grad[X, 0], grad[X, 1]
         tmp32[X, pl.ds(0, tok, stride=2), :] = jnp.where(core == 0, own, other)
         tmp32[X, pl.ds(1, tok, stride=2), :] = jnp.where(core == 0, other, own)
-        out[...] = tmp32[X].astype(jnp.bfloat16)
-    for c in sends:
-        c.wait_send()
-    for x in x_out:
-        x.wait_recv()
+        outb[X] = tmp32[X].astype(jnp.bfloat16)
+        store(outb.at[X], out, 2 + X)
+    for ref, sem in ((rbuf.at[0], ag_send), (rbuf, rs_send), (dpbuf.at[0], pair_send.at[0])):
+        remote(ref, ref, sem, sem, to_partner).wait_send()
+    x_lse[0].wait_send()
+    remote(ost, ost, pair_send.at[0], pair_recv.at[2], to_partner).wait_recv()
+    for c in local:
+        c.wait()
     scope_out.__exit__(None, None, None)
 
 
-def store_kernel(o_in, lse_in, dq_in, dk_in, dv_in, o_out, lse_out, dq_out, dk_out, dv_out, lse_v, sem):
-    copies = [pltpu.make_async_copy(a, b, sem.at[i]) for i, (a, b) in enumerate(
-        ((o_in, o_out), (dq_in, dq_out), (dk_in, dk_out), (dv_in, dv_out), (lse_v, lse_out)))]
-    for c in copies[:4]:
+def store_kernel(*refs):
+    n = len(refs) // 2
+    copies = [pltpu.make_async_copy(refs[i], refs[n + i], refs[-1].at[i]) for i in range(n)]
+    for c in copies:
         c.start()
-    grp = lse_in.shape[1]
-    for i in range(lse_in.shape[0]):
-        lse_v[i * grp:(i + 1) * grp, :] = lse_in[i]
-    copies[4].start()
     for c in copies:
         c.wait()
 
@@ -472,7 +508,7 @@
         assert kvh == CORES and cp == CORES * SIDE * SIDE and keys == hd
         bf, f32 = jnp.bfloat16, jnp.float32
         hbm_spec = pl.BlockSpec(memory_space=pltpu.HBM)
-        vmem_spec = pl.BlockSpec(memory_space=pltpu.VMEM)
+        any_spec = pl.BlockSpec(memory_space=pl.ANY)
         n_rs = len(RIDX)
         flat = lambda x: x.reshape(tok * kvh, hd)
         o, lse, dq, dk, dv = pl.pallas_call(
@@ -480,13 +516,13 @@
             name='ring_attention',
             out_shape=[
                 jax.ShapeDtypeStruct((heads, tok, hd), bf),
-                jax.ShapeDtypeStruct((CORES, grp, tok), f32),
+                jax.ShapeDtypeStruct((heads, tok), f32),
                 jax.ShapeDtypeStruct((heads, tok, hd), bf),
                 jax.ShapeDtypeStruct((tok * kvh, hd), bf),
                 jax.ShapeDtypeStruct((tok * kvh, hd), bf),
             ],
             in_specs=[hbm_spec] * 6,
-            out_specs=[vmem_spec] * 5,
+            out_specs=[any_spec] * 5,
             scratch_shapes=[
                 pltpu.VMEM((2, tok * kvh, hd), bf),
                 pltpu.VMEM((2, tok * kvh, hd), f32),
@@ -504,12 +540,13 @@
                 pltpu.VMEM((NBLK, keys, rows), bf),
                 pltpu.VMEM((2, NBLK, CORES, tok, hd), f32),
                 pltpu.VMEM((2, n_rs, tok, hd), f32),
-                pltpu.VMEM((grp, tok, hd), bf),
-                pltpu.VMEM((grp, tok, hd), bf),
-                pltpu.VMEM((grp, tok), f32),
-                pltpu.VMEM((2, tok, hd), f32),
+                pltpu.VMEM((heads, tok, hd), bf),
+                pltpu.VMEM((heads, tok, hd), bf),
+                pltpu.VMEM((CORES + 1, grp, tok), f32),
                 pltpu.VMEM((2, 2, tok, hd), f32),
                 pltpu.VMEM((2, tok * kvh, hd), f32),
+                pltpu.VMEM((2, tok * kvh, hd), bf),
+                pltpu.VMEM((heads, tok), f32),
                 pltpu.VMEM((1, rows), f32),
                 pltpu.VMEM((1, rows), f32),
                 pltpu.VMEM((1, rows), f32),
@@ -519,13 +556,13 @@
                 pltpu.VMEM((hd, rows), f32),
                 pltpu.VMEM((1, tok), jnp.int32),
                 pltpu.SMEM((1, n_docs + 1), jnp.int32),
-                pltpu.SemaphoreType.DMA((6,)),
-                pltpu.SemaphoreType.DMA((9,)),
-                pltpu.SemaphoreType.DMA((9,)),
-                pltpu.SemaphoreType.DMA((64,)),
-                pltpu.SemaphoreType.DMA((2, NBLK, CORES)),
-                pltpu.SemaphoreType.DMA((2, n_rs)),
-                pltpu.SemaphoreType.DMA((2, n_rs)),
+                pltpu.SemaphoreType.DMA((5,)),
+                pltpu.SemaphoreType.DMA((2,)),
+                pltpu.SemaphoreType.DMA((4,)),
+                pltpu.SemaphoreType.DMA(()),
+                pltpu.SemaphoreType.DMA((len(AIDX),)),
+                pltpu.SemaphoreType.DMA(()),
+                pltpu.SemaphoreType.DMA((2, len(RSEM))),
             ],
             compiler_params=pltpu.CompilerParams(
                 collective_id=0, has_side_effects=True, vmem_limit_bytes=40 * 1024 * 1024),
@@ -540,9 +577,9 @@
                 jax.ShapeDtypeStruct((tok * kvh, hd), bf),
                 jax.ShapeDtypeStruct((tok * kvh, hd), bf),
             ],
-            in_specs=[vmem_spec] * 5,
+            in_specs=[any_spec] * 5,
             out_specs=[hbm_spec] * 5,
-            scratch_shapes=[pltpu.VMEM((heads, tok), f32), pltpu.SemaphoreType.DMA((5,))],
+            scratch_shapes=[pltpu.SemaphoreType.DMA((5,))],
             compiler_params=pltpu.CompilerParams(vmem_limit_bytes=1024 * 1024),
         )(o, lse, dq, dk, dv)
         back = lambda x: x.reshape(tok, kvh, hd)

time: 37.2 us -> 35.8 us (0.962)
  Pallas kernels: 36.4 us -> 35 us
    pallas_call x1, Pallas kernels: 35.6 us -> 34.2 us  [local(): pl.pallas_call(functools.partial(kernel, cp, n_docs, hd ** (-0.5)), name=...]
where the time goes in v5:
time: 35.8 us; the launch traced here: 35.7 us
  Pallas kernels  35 us (98%)
  between operations  0.64 us (2%)
    pallas_call x1, Pallas kernels, local(): pl.pallas_call(functools.partial(kernel, cp, n_docs, hd ** (-0.5)), name=...  34.2 us
    pallas_call x1, Pallas kernels, local(): pl.pallas_call(store_kernel, name='store_outputs', out_shape=[jax.ShapeDt...  0.81 us

profile of v5, /device:TPU:97, one launch (start us, length us, event | category | flops | bytes accessed | tf_op | source)
XLA Modules:
  0.0 35.7 jit_solution(16914420623514431895)
XLA Ops:
  0.6 34.2 %ring_attention.1 = (bf16[12,64,128]{2,1,0:T(8,128)(2,1)S(1)}, f32[12,64]{1,0:T(8,128)S(1)}, bf16[12,64,128]{2,1,0:T(8,128)(2,1)S(1)}, bf16[128,128]{1,0:T(8,128)(2,1)S(1)}, bf16[128,128]{1,0:T(8,128)(2,1)S(1)}) custom-call(bf16[12,64,128]{2,1,0:T(8,128)(2,1)} %bitcast.11, bf16[128,128]{1,0:T(8,128)(2,1)} %bitcast.13, bf16[128,128]{1,0:T(8,128)(2,1)} %bitcast.14, ...), custom_call_target="tpu_custom_call" | custom-call | tf_op jit(solution)/shard_map/ring_attention/pallas_call | solution.py:514
  34.8 0.8 %store_outputs.1 = (bf16[12,64,128]{2,1,0:T(8,128)(2,1)}, f32[12,64]{1,0:T(8,128)}, bf16[12,64,128]{2,1,0:T(8,128)(2,1)}, bf16[128,128]{1,0:T(8,128)(2,1)}, bf16[128,128]{1,0:T(8,128)(2,1)}) custom-call(bf16[12,64,128]{2,1,0:T(8,128)(2,1)S(1)} %get-tuple-element.15.refs_0_, f32[12,64]{1,0:T(8,128)S(1)} %get-tuple-element.16.refs_1_, ...), custom_call_target="tpu_custom_call" | custom-call | tf_op jit(solution)/shard_map/store_outputs/pallas_call | solution.py:570

commit v6 on v5

--- a/solution.py
+++ b/solution.py
@@ -49,11 +49,11 @@
 
 RELAYED = ()
 ORDER = tuple(all_tasks()[i] for i in dict.fromkeys(b for n in (
-    0x112f200f022d011e2e1f, 0x00103c12140523313213, 0x3d30032104221a191837, 0x380b29280a27093e360e,
-    0x3b081d262c3517344546, 0x47071c0d0c162b061b15, 0x413f25393a2a3324404b, 0x4d4c484a4942434e5a93,
-    0x65835e619271825b7984, 0x5c9462725d739a866353, 0x59589574445754649c87, 0x8556666955888b969775,
-    0x7b8c9b8a67985f6a5076, 0x516b777a4f7c52606c78, 0x68999d8d89908f9f6d8e, 0x7d9e6e6f7ea07fa18091,
-    0x8170a2a2a2a2a2a2a2a2,
+    0x112f02200f2e10002d01, 0x1f1e3e31052314320422, 0x03133021123c181a0829, 0x0b38090e282c26171d35,
+    0x3d190a3b274536461b37, 0x47240c063a151c3f342b, 0x070d39252a164033414b, 0x4d4c48494a42434e5e71,
+    0x9282615c72865a658362, 0x935d63739a5b79948459, 0x74586485954457567b54, 0x669b5296535576978a9c,
+    0x7a87756a50986b697788, 0x8b674f518c7c9d997860, 0x9f7e7d899e7f8f68a06d, 0x8d906e8e6c6f5f80a191,
+    0x81a27070707070707070,
 ) for b in n.to_bytes(10, 'big')))
 NT = (((1,), (1,)), ((), ()))
 TN = (((0,), (0,)), ((), ()))

time: 35.8 us -> 34.3 us (0.958)
  Pallas kernels: 35 us -> 33.6 us
    pallas_call x1, Pallas kernels: 34.2 us -> 32.7 us  [local(): pl.pallas_call(functools.partial(kernel, cp, n_docs, hd ** (-0.5)), name=...]
where the time goes in v6:
time: 34.3 us; the launch traced here: 34.2 us
  Pallas kernels  33.6 us (98%)
  between operations  0.64 us (2%)
    pallas_call x1, Pallas kernels, local(): pl.pallas_call(functools.partial(kernel, cp, n_docs, hd ** (-0.5)), name=...  32.7 us
    pallas_call x1, Pallas kernels, local(): pl.pallas_call(store_kernel, name='store_outputs', out_shape=[jax.ShapeDt...  0.81 us

profile of v6, /device:TPU:97, one launch (start us, length us, event | category | flops | bytes accessed | tf_op | source)
XLA Modules:
  0.0 34.2 jit_solution(11839833179835157654)
XLA Ops:
  0.6 32.7 %ring_attention.1 = (bf16[12,64,128]{2,1,0:T(8,128)(2,1)S(1)}, f32[12,64]{1,0:T(8,128)S(1)}, bf16[12,64,128]{2,1,0:T(8,128)(2,1)S(1)}, bf16[128,128]{1,0:T(8,128)(2,1)S(1)}, bf16[128,128]{1,0:T(8,128)(2,1)S(1)}) custom-call(bf16[12,64,128]{2,1,0:T(8,128)(2,1)} %bitcast.11, bf16[128,128]{1,0:T(8,128)(2,1)} %bitcast.13, bf16[128,128]{1,0:T(8,128)(2,1)} %bitcast.14, ...), custom_call_target="tpu_custom_call" | custom-call | tf_op jit(solution)/shard_map/ring_attention/pallas_call | solution.py:514
  33.4 0.8 %store_outputs.1 = (bf16[12,64,128]{2,1,0:T(8,128)(2,1)}, f32[12,64]{1,0:T(8,128)}, bf16[12,64,128]{2,1,0:T(8,128)(2,1)}, bf16[128,128]{1,0:T(8,128)(2,1)}, bf16[128,128]{1,0:T(8,128)(2,1)}) custom-call(bf16[12,64,128]{2,1,0:T(8,128)(2,1)S(1)} %get-tuple-element.15.refs_0_, f32[12,64]{1,0:T(8,128)S(1)} %get-tuple-element.16.refs_1_, ...), custom_call_target="tpu_custom_call" | custom-call | tf_op jit(solution)/shard_map/store_outputs/pallas_call | solution.py:570
